TPU v7x, 256 devices: a whole 4x4x8 slice. The times are simulated.
256 devices in a mesh: ta: 32 (over z, y_lo, core), gz: 4 (over x), gy: 2 (over y_hi).
Axes of the slice: x: 4, y: 4 (y_hi: 2, y_lo: 2; y = y_hi * 2 + y_lo), z: 8, core: 2. Of those that a mesh axis runs over, the one named last changes fastest.
Arguments:
- right_side: float32 [256, 32, 32, 128], P('ta', 'gz', 'gy'), may hold values from -12 to 12, as said below
- mass_field: float32 [256, 32, 32, 128], P('ta', 'gz', 'gy'), may hold values from 0.05 to 0.8
Outputs:
- solution: float32 [256, 32, 32, 128], P('ta', 'gz', 'gy')
- residual: float32 [256, 32, 32, 128], P('ta', 'gz', 'gy')
Inputs may be any that keep to these rules, and one draw needn't show every extreme that they name: right_side is twice a field constant on aligned blocks of 8 x 8 x 8 x 8 sites plus site-by-site noise, each part within -4 to 4.
All inputs are finite; a program needn't handle non-finite values.
Results may differ from a plain program's by a relative error of at most 0.0003.
Values sent between devices are 32-bit elements.
A program may use at most 128 MiB of HBM per device.

v0:
```python
import functools

import jax
import jax.numpy as jnp
from jax import lax
from jax.experimental import pallas as pl
from jax.experimental.pallas import tpu as pltpu
from jax.sharding import PartitionSpec as P

DAMPING = 0.7
KEEP = 1.0 - DAMPING
MESH = pl.DeviceIdType.MESH


def rolled(values, shift, axis):
    return pltpu.roll(values, shift % values.shape[axis], axis)


def pair_swap(values, step, axis):
    index = lax.broadcasted_iota(jnp.int32, values.shape, axis)
    return jnp.where((index // step) % 2 == 0, rolled(values, -step, axis), rolled(values, step, axis))


def z_pairs(summed):
    count, rows, lanes = summed.shape
    summed = summed.reshape(count // 2, 2, rows, lanes)
    return summed[:, 0] + summed[:, 1]


def refined_z(slab):
    return jnp.repeat(slab, 2, axis=0)


def shifted_z(slab, forward):
    if forward:
        return jnp.concatenate([slab[-1:], slab[:-1]], axis=0)
    return jnp.concatenate([slab[1:], slab[:1]], axis=0)


def kernel(sizes, s_hbm, m_hbm, sol_ref, res_ref, *scratch):
    nta, ngz, ngy = sizes
    (g0, v0a, v0b, v0w, v0x, v0s, y0, ys0, fold,
     s1, m1, g1, v1a, v1b, v1w, v1x, e1, e2,
     mall, rall, s2, m2, g2, u2, w2,
     f0s, f0r, f1s, f1r, fxs, fxr, gsend, grecv, s_ref, m_ref, loaded) = scratch
    size_t, size_z, rows, lanes = s_ref.shape
    size_t1, size_z1, rows1 = size_t // 2, size_z // 2, rows // 2
    part_t, part_z, rows2 = size_t // 4, size_z // 4, rows // 4
    all_t, all_z = part_t * nta, part_z * ngz
    ta, gz, gy = lax.axis_index("ta"), lax.axis_index("gz"), lax.axis_index("gy")

    first_up = lax.min(ta, 1)

    def device(dt, dz, dy):
        return {
            "ta": lax.rem(ta + dt + nta, nta),
            "gz": lax.rem(gz + dz + ngz, ngz),
            "gy": lax.rem(gy + dy + ngy, ngy),
        }

    near = [(dt, dz, dy) for dt in (-1, 0, 1) for dz in (-1, 0, 1) for dy in range(ngy)]
    across = [(dt, dz, 0) for dt in reversed(range(nta)) for dz in range(ngz) if dt or dz]
    loads = []
    for t in range(size_t):
        loads.append((
            pltpu.make_async_copy(m_hbm.at[pl.ds(t, 1)], m_ref.at[pl.ds(t, 1)], loaded.at[0, t]),
            pltpu.make_async_copy(s_hbm.at[pl.ds(t, 1)], s_ref.at[pl.ds(t, 1)], loaded.at[1, t]),
        ))
    met = sorted({(dt % nta, dz % ngz, dy % ngy) for dt, dz, dy in near + across} - {(0, 0, 0)})
    barrier = pltpu.get_barrier_semaphore()
    for offset in met:
        pl.semaphore_signal(barrier, inc=1, device_id=device(*offset), device_id_type=MESH)
    for t in [0, size_t - 1] + list(range(1, size_t - 1)):
        for load in loads[t]:
            load.start()

    def send(moves, sends, receives):
        copies = [
            pltpu.make_async_remote_copy(
                src_ref=source, dst_ref=target, send_sem=sends(place), recv_sem=receives(place),
                device_id=device(*offset), device_id_type=MESH,
            )
            for place, source, target, offset in moves
        ]
        for copy in copies:
            copy.start()
        sent.extend(copies)
        return copies

    def finish(copies):
        for copy in copies:
            copy.wait_recv()

    sent = []

    def finish_sends(copies):
        for copy in copies:
            copy.wait_send()

    inner_t, inner_z = pl.ds(1, size_t), pl.ds(1, size_z)

    def send0(number, moves):
        return send(moves, lambda place: f0s.at[number, place], lambda place: f0r.at[number, place])

    def exchange_t(number, field):
        moves = []
        for up in (first_up, 1 - first_up):
            here, there = pl.ds(1 + (size_t - 1) * up, 1), pl.ds((size_t + 1) * (1 - up), 1)
            moves.append((up, field.at[here, inner_z], field.at[there, inner_z], (2 * up - 1, 0, 0)))
        return send0(number, moves)

    def exchange_sides(number, field, faces, halos):
        return send0(number, [
            (2, field.at[inner_t, pl.ds(size_z, 1)], field.at[inner_t, pl.ds(0, 1)], (0, 1, 0)),
            (3, field.at[inner_t, pl.ds(1, 1)], field.at[inner_t, pl.ds(size_z + 1, 1)], (0, -1, 0)),
            (4, faces.at[1], halos.at[0], (0, 0, 1)),
            (5, faces.at[0], halos.at[1], (0, 0, -1)),
        ])

    def around(field, part, dys):
        own_t, own_z = pl.ds(2, size_t1), pl.ds(2, size_z1)

        def span(size, deep, up):
            return pl.ds(2 + (size - deep) * up, deep), pl.ds(2 + size - (size + deep) * up, deep)

        moves = []
        for up in (first_up, 1 - first_up):
            here, there = span(size_t1, 2, up)
            for dy in dys:
                moves.append((
                    8 * dy + up, field.at[(here, own_z) + part], field.at[(there, own_z) + part],
                    (2 * up - 1, 0, dy),
                ))
        for up in (1, 0):
            here_t, there_t = span(size_t1, 1, up)
            for up_z in (1, 0):
                here_z, there_z = span(size_z1, 1, up_z)
                for dy in dys:
                    moves.append((
                        8 * dy + 2 + 2 * up + up_z,
                        field.at[(here_t, here_z) + part], field.at[(there_t, there_z) + part],
                        (2 * up - 1, 2 * up_z - 1, dy),
                    ))
        for up in (1, 0):
            here, there = span(size_z1, 2, up)
            for dy in dys:
                moves.append((
                    8 * dy + 6 + up, field.at[(own_t, here) + part], field.at[(own_t, there) + part],
                    (0, 2 * up - 1, dy),
                ))
        return moves

    def spread1(number, field):
        own = field.at[pl.ds(2, size_t1), pl.ds(2, size_z1), pl.ds(gy, 1)]
        moves = around(field, (pl.ds(gy, 1),), range(ngy))
        moves += [(8 * ngy + dy - 1, own, own, (0, 0, dy)) for dy in range(1, ngy)]
        return send(moves, lambda place: f1s.at[number, place], lambda place: f1r.at[number, place])

    def gather(number, field):
        own = field.at[ta, gz]
        return send(
            [(place, own, own, offset) for place, offset in enumerate(across)],
            lambda place: gsend.at[number, place], lambda place: grecv.at[number, place],
        )

    def put(field, faces, t, slab):
        field[t + 1, pl.ds(1, size_z)] = slab
        faces[0, t] = slab[:, :1]
        faces[1, t] = slab[:, rows - 1:]

    def sum0(field, halos, t):
        slab = field[t + 1, pl.ds(1, size_z)]
        row = lax.broadcasted_iota(jnp.int32, slab.shape, 1)
        summed = field[t, pl.ds(1, size_z)] + field[t + 2, pl.ds(1, size_z)]
        summed = summed + field[t + 1, pl.ds(0, size_z)] + field[t + 1, pl.ds(2, size_z)]
        summed = summed + jnp.where(row == 0, halos[0, t], rolled(slab, 1, 1))
        summed = summed + jnp.where(row == rows - 1, halos[1, t], rolled(slab, -1, 1))
        return slab, summed + rolled(slab, 1, 2) + rolled(slab, -1, 2)

    def halved(summed, place, step):
        count, high, _ = summed.shape
        view = fold.at[place, pl.ds(0, count)]
        view[...] = summed
        summed = view[:, pl.ds(0, high // 2, stride=2), :] + view[:, pl.ds(1, high // 2, stride=2), :]
        return (summed + pair_swap(summed, step, 2)) * 0.0625

    def doubled(slab, place):
        count, high, _ = slab.shape
        view = fold.at[place, pl.ds(0, count)]
        view[:, pl.ds(0, high, stride=2), :] = slab
        view[:, pl.ds(1, high, stride=2), :] = slab
        return view[...]

    full = ngy * rows1

    def near1(radius):
        for a in range(2 - radius, 2 + size_t1 + radius):
            reach = radius - max(2 - a, a - 1 - size_t1, 0)
            yield a, 2 - reach, size_z1 + 2 * reach

    def read1(field, a, b, count):
        return field[a, pl.ds(b, count)].reshape(count, full, lanes)

    def write1(field, a, b, slab):
        field[a, pl.ds(b, slab.shape[0])] = slab.reshape(slab.shape[0], ngy, rows1, lanes)

    def sum1(field, a, b, count):
        slab = read1(field, a, b, count)
        summed = read1(field, a - 1, b, count) + read1(field, a + 1, b, count)
        summed = summed + read1(field, a, b - 1, count) + read1(field, a, b + 1, count)
        summed = summed + rolled(slab, 1, 1) + rolled(slab, -1, 1)
        return slab, summed + rolled(slab, 2, 2) + rolled(slab, -2, 2)

    def sweep1(field, out, radius):
        for a, b, count in near1(radius):
            slab, summed = sum1(field, a, b, count)
            fresh = KEEP * slab + read1(g1, a, b, count) * (read1(s1, a, b, count) + 0.5 * summed)
            write1(out, a, b, fresh)

    def packed(out, slabs):
        parts = [slab[z] for slab in slabs for z in range(part_z)]
        lane = lax.broadcasted_iota(jnp.int32, parts[0].shape, 1)
        values = parts[0]
        for k in range(1, len(parts)):
            values = jnp.where(lane % 4 == k, parts[k], values)
        out[ta, gz] = values

    def unpacked(source, t):
        pair, odd = divmod(t, part_t)
        values = source[pair]
        lane = lax.broadcasted_iota(jnp.int32, values.shape, 2)
        pieces = []
        for z in range(part_z):
            piece = jnp.where(lane % 4 == odd * part_z + z, values, 0.0)
            piece = piece + pair_swap(piece, 1, 2)
            pieces.append(piece + pair_swap(piece, 2, 2))
        return jnp.stack(pieces, axis=1).reshape(all_z, ngy * rows2, lanes)

    inside = list(range(1, size_t - 1))
    ends = [0, size_t - 1]

    def first0(ts):
        for t in ts:
            for load in loads[t]:
                load.wait()
            weight = DAMPING / (8.0 + m_ref[t])
            g0[t] = weight
            put(v0a, ys0.at[0], t, weight * s_ref[t])

    first0(ends + inside)
    pl.semaphore_wait(barrier, len(met))
    over_t = exchange_t(0, v0a)
    sides = exchange_sides(0, v0a, ys0.at[0], y0.at[0])
    for t in range(size_t1):
        mean = halved(z_pairs(m_ref[2 * t] + m_ref[2 * t + 1]), t, 1)
        m1[t + 2, pl.ds(2, size_z1), gy] = mean
    mass_copies = spread1(0, m1)

    def sweep0(field, halos, out, faces, ts, also=None):
        for t in ts:
            slab, summed = sum0(field, halos, t)
            fresh = KEEP * slab + g0[t] * (s_ref[t] + summed)
            put(out, faces, t, fresh)
            if also is not None:
                also[t] = fresh

    finish(sides)
    sweep0(v0a, y0.at[0], v0b, ys0.at[1], inside)
    finish(over_t)
    sweep0(v0a, y0.at[0], v0b, ys0.at[1], ends)
    over_t = exchange_t(1, v0b)
    sides = exchange_sides(1, v0b, ys0.at[1], y0.at[1])
    finish(mass_copies)
    for a, b, count in near1(2):
        write1(g1, a, b, DAMPING / (4.0 + read1(m1, a, b, count)))

    def to_level2(slabs):
        return [
            halved(z_pairs(slabs[2 * t] + slabs[2 * t + 1]), t, 2) for t in range(part_t)
        ]

    packed(mall, to_level2([read1(m1, 2 + t, 2, size_z1) for t in range(size_t1)]))
    mass_copies = gather(0, mall)

    def remainder0(ts):
        for t in ts:
            remainder = []
            for odd in range(2):
                slab, summed = sum0(v0b, y0.at[1], 2 * t + odd)
                remainder.append(s_ref[2 * t + odd] + summed - (8.0 + m_ref[2 * t + odd]) * slab)
            s1[t + 2, pl.ds(2, size_z1), gy] = halved(z_pairs(remainder[0] + remainder[1]), t, 1)

    finish(sides)
    remainder0(range(1, size_t1 - 1))
    finish(over_t)
    remainder0((0, size_t1 - 1))
    source_copies = spread1(1, s1)
    finish(mass_copies)
    for t in range(all_t):
        mass = unpacked(mall, t)
        m2[t] = mass
        g2[t] = DAMPING / (2.0 + mass)
    weights3 = [
        DAMPING / (1.0 + coarse_full(m2[2 * t], m2[2 * t + 1])) for t in range(all_t // 2)
    ]
    finish(source_copies)

    for a, b, count in near1(2):
        write1(v1a, a, b, read1(g1, a, b, count) * read1(s1, a, b, count))
    sweep1(v1a, v1b, 1)
    remainder = []
    for a, b, count in near1(0):
        slab, summed = sum1(v1b, a, b, count)
        remainder.append(
            read1(s1, a, b, count) + 0.5 * summed - (4.0 + read1(m1, a, b, count)) * slab
        )
    packed(rall, to_level2(remainder))
    finish(gather(1, rall))

    for t in range(all_t):
        source = unpacked(rall, t)
        s2[t] = source
        u2[t] = g2[t] * source

    def sum2(field, t):
        slab = field[t]
        summed = field[(t - 1) % all_t] + field[(t + 1) % all_t]
        summed = summed + shifted_z(slab, True) + shifted_z(slab, False)
        summed = summed + rolled(slab, 1, 1) + rolled(slab, -1, 1)
        return slab, summed + rolled(slab, 4, 2) + rolled(slab, -4, 2)

    def sweep2(field, out):
        for t in range(all_t):
            slab, summed = sum2(field, t)
            out[t] = KEEP * slab + g2[t] * (s2[t] + 0.25 * summed)

    sweep2(u2, w2)
    sources3 = []
    for t in range(all_t // 2):
        remainder = []
        for odd in range(2):
            slab, summed = sum2(w2, 2 * t + odd)
            remainder.append(s2[2 * t + odd] + 0.25 * summed - (2.0 + m2[2 * t + odd]) * slab)
        sources3.append(coarse_full(*remainder))

    values = [weight * source for weight, source in zip(weights3, sources3)]
    count = len(values)
    for sweep_no in range(3):
        fresh = []
        for t in range(count):
            slab = values[t]
            summed = values[(t - 1) % count] + values[(t + 1) % count]
            summed = summed + shifted_z(slab, True) + shifted_z(slab, False)
            summed = summed + rolled(slab, 2, 1) + rolled(slab, -2, 1)
            summed = summed + rolled(slab, 8, 2) + rolled(slab, -8, 2)
            fresh.append(KEEP * slab + weights3[t] * (sources3[t] + 0.125 * summed))
        values = fresh

    for t in range(all_t):
        w2[t] = w2[t] + refined_z(values[t // 2])
    sweep2(w2, u2)
    sweep2(u2, w2)

    for a in range(part_t + 2):
        at_t = lax.rem(ta * part_t + (a - 1 + all_t), all_t)
        slabs = []
        for b in range(part_z + 2):
            at_z = lax.rem(gz * part_z + (b - 1 + all_z), all_z)
            slabs.append(w2[at_t, pl.ds(at_z, 1)])
        e2[a] = doubled(jnp.concatenate(slabs, axis=0), a)
    for a, b, count in near1(1):
        fine = refined_z(e2[a // 2])
        write1(v1w, a, b, read1(v1b, a, b, count) + fine[b:b + count])
    sweep1(v1w, v1x, 0)
    finish(send(
        around(v1x, (), (0,)), lambda place: fxs.at[place], lambda place: fxr.at[place],
    ))
    sweep1(v1x, e1, 1)

    under = lax.rem(gy + ngy - 1, ngy)
    over = lax.rem(gy + 1, ngy)
    def corrected0(layers):
        for at_t in layers:
            own = [p for p in (2 * at_t - 3, 2 * at_t - 2) if 1 <= p <= size_t]
            if not own:
                p = 0 if at_t == 1 else size_t + 1
                fine = refined_z(doubled(e1[at_t, pl.ds(2, size_z1), gy], 0))
                v0w[p, inner_z] = v0b[p, inner_z] + fine
                continue
            fine = refined_z(doubled(e1[at_t, pl.ds(1, size_z1 + 2), gy], at_t % 4))
            fine = fine[1:1 + size_z + 2]
            low = refined_z(e1[at_t, pl.ds(2, size_z1), under, pl.ds(rows1 - 1, 1)])
            high = refined_z(e1[at_t, pl.ds(2, size_z1), over, pl.ds(0, 1)])
            for p in own:
                v0w[p] = v0b[p] + fine
                y0[2, 0, p - 1] = y0[1, 0, p - 1] + low
                y0[2, 1, p - 1] = y0[1, 1, p - 1] + high

    corrected0((1, 2, size_t1 + 1, size_t1 + 2))
    sweep0(v0w, y0.at[2], v0x, ys0.at[2], ends)
    over_t = exchange_t(2, v0x)
    corrected0(range(3, size_t1 + 1))
    sweep0(v0w, y0.at[2], v0x, ys0.at[2], inside)
    sides = exchange_sides(2, v0x, ys0.at[2], y0.at[3])
    finish(sides)
    sweep0(v0x, y0.at[3], v0s, ys0.at[3], inside, sol_ref)
    finish(over_t)
    sweep0(v0x, y0.at[3], v0s, ys0.at[3], ends, sol_ref)
    earlier = len(sent)
    over_t = exchange_t(3, v0s)
    sides = exchange_sides(3, v0s, ys0.at[3], y0.at[4])
    finish_sends(sent[:earlier])

    def residual(ts):
        for t in ts:
            slab, summed = sum0(v0s, y0.at[4], t)
            res_ref[t] = s_ref[t] + summed - (8.0 + m_ref[t]) * slab

    finish(sides)
    residual(inside)
    finish(over_t)
    residual(ends)
    finish_sends(sent[earlier:])


def coarse_full(even, odd):
    summed = even + odd
    count, rows, lanes = summed.shape
    summed = summed.reshape(count // 2, 2, rows, lanes)
    summed = summed[:, 0] + summed[:, 1]
    summed = summed + pair_swap(summed, 1, 1)
    return (summed + pair_swap(summed, 4, 2)) * 0.0625


def per_device(sizes, right_side, mass_field):
    nta, ngz, ngy = sizes
    size_t, size_z, rows, lanes = right_side.shape
    size_t1, size_z1, rows1 = size_t // 2, size_z // 2, rows // 2
    part_t, part_z, rows2 = size_t // 4, size_z // 4, rows // 4
    vmem = lambda *shape: pltpu.VMEM(shape, jnp.float32)
    dma = lambda *shape: pltpu.SemaphoreType.DMA(shape)
    padded0 = vmem(size_t + 2, size_z + 2, rows, lanes)
    padded1 = vmem(size_t1 + 4, size_z1 + 4, ngy, rows1, lanes)
    whole2 = vmem(part_t * nta, part_z * ngz, rows2 * ngy, lanes)
    packs = vmem(nta, ngz, rows2 * ngy, lanes)
    spreads, peers = 8 * ngy + ngy - 1, nta * ngz - 1
    scratch = [
        vmem(size_t, size_z, rows, lanes), padded0, padded0, padded0, padded0, padded0,
        vmem(5, 2, size_t, size_z, 1, lanes), vmem(4, 2, size_t, size_z, 1, lanes),
        vmem(max(size_t1, part_t + 2), size_z, max(rows, ngy * rows1), lanes),
        *[padded1] * 8, vmem(part_t + 2, part_z + 2, ngy * rows1, lanes),
        packs, packs, *[whole2] * 5,
        dma(4, 6), dma(4, 6), dma(2, spreads), dma(2, spreads), dma(8), dma(8),
        dma(2, peers), dma(2, peers),
        vmem(size_t, size_z, rows, lanes), vmem(size_t, size_z, rows, lanes), dma(2, size_t),
    ]
    block = jax.ShapeDtypeStruct(right_side.shape, jnp.float32)
    return pl.pallas_call(
        functools.partial(kernel, sizes),
        out_shape=(block, block),
        in_specs=[pl.BlockSpec(memory_space=pltpu.HBM)] * 2,
        out_specs=(pl.BlockSpec(memory_space=pltpu.VMEM),) * 2,
        scratch_shapes=scratch,
        compiler_params=pltpu.CompilerParams(
            collective_id=0, has_side_effects=True, vmem_limit_bytes=48 * 1024 * 1024
        ),
    )(right_side, mass_field)


def solution(mesh):
    sizes = tuple(mesh.shape[axis] for axis in ("ta", "gz", "gy"))
    spec = P("ta", "gz", "gy", None)
    return jax.shard_map(
        functools.partial(per_device, sizes),
        mesh=mesh,
        in_specs=(spec, spec),
        out_specs=(spec, spec),
        check_vma=False,
    )
```

profile of v0, /device:TPU:33, one launch (start us, length us, event | category | flops | bytes accessed | tf_op | source)
XLA Modules:
  0.0 109.2 jit_solution(8678190749038239674)
XLA Ops:
  0.6 0.0 copy-start
  0.6 1.0 copy-done
  1.7 0.0 copy-start.1
  1.7 1.0 copy-done.1
  2.7 104.9 %shard_map.41 = (f32[8,8,16,128]{3,2,1,0:T(8,128)S(1)}, f32[8,8,16,128]{3,2,1,0:T(8,128)S(1)}) custom-call(f32[8,8,16,128]{3,2,1,0:T(8,128)S(1)} %copy-done, f32[8,8,16,128]{3,2,1,0:T(8,128)S(1)} %copy-done.1), custom_call_target="tpu_custom_call" | custom-call | tf_op jit(solution)/shard_map/pallas_call | solution.py:458
  107.6 0.8 copy.6
  108.4 0.8 copy.7
Async XLA Ops:
  0.6 1.0 copy-start
  1.7 1.0 copy-start.1
where the time goes:
time: 109 us
  Pallas kernels  105 us (96%)
  local copies, waits for them, and re-layouts  3.66 us (3%)
    pallas_call x1, Pallas kernels, per_device(): pl.pallas_call(functools.partial(kernel, sizes), out_shape=(block, block)...  105 us
    unnamed x6, local copies, waits for them, and re-layouts  3.66 us

commit v1 on v0

--- a/solution.py
+++ b/solution.py
@@ -41,12 +41,13 @@
     nta, ngz, ngy = sizes
     (g0, v0a, v0b, v0w, v0x, v0s, y0, ys0, fold,
      s1, m1, g1, v1a, v1b, v1w, v1x, e1, e2,
-     mall, rall, s2, m2, g2, u2, w2,
+     m2, s2, g2, u2, w2, m3, s3,
      f0s, f0r, f1s, f1r, fxs, fxr, gsend, grecv, s_ref, m_ref, loaded) = scratch
     size_t, size_z, rows, lanes = s_ref.shape
     size_t1, size_z1, rows1 = size_t // 2, size_z // 2, rows // 2
     part_t, part_z, rows2 = size_t // 4, size_z // 4, rows // 4
-    all_t, all_z = part_t * nta, part_z * ngz
+    stages = plan(nta, ngz)
+    slots = {cell: number for number, cell in enumerate(stages["source"])}
     ta, gz, gy = lax.axis_index("ta"), lax.axis_index("gz"), lax.axis_index("gy")
 
     first_up = lax.min(ta, 1)
@@ -59,14 +60,18 @@
         }
 
     near = [(dt, dz, dy) for dt in (-1, 0, 1) for dz in (-1, 0, 1) for dy in range(ngy)]
-    across = [(dt, dz, 0) for dt in reversed(range(nta)) for dz in range(ngz) if dt or dz]
+    centred = lambda d, n: (d + n // 2) % n - n // 2
+    across = sorted(
+        (cell for cell in slots if cell != (0, 0)),
+        key=lambda c: -(abs(centred(c[0], nta)) + 2 * abs(centred(c[1], ngz))),
+    )
     loads = []
     for t in range(size_t):
         loads.append((
             pltpu.make_async_copy(m_hbm.at[pl.ds(t, 1)], m_ref.at[pl.ds(t, 1)], loaded.at[0, t]),
             pltpu.make_async_copy(s_hbm.at[pl.ds(t, 1)], s_ref.at[pl.ds(t, 1)], loaded.at[1, t]),
         ))
-    met = sorted({(dt % nta, dz % ngz, dy % ngy) for dt, dz, dy in near + across} - {(0, 0, 0)})
+    met = sorted({(dt % nta, dz % ngz, dy % ngy) for dt, dz, dy in near + [(-t, -z, 0) for t, z in across]} - {(0, 0, 0)})
     barrier = pltpu.get_barrier_semaphore()
     for offset in met:
         pl.semaphore_signal(barrier, inc=1, device_id=device(*offset), device_id_type=MESH)
@@ -157,9 +162,9 @@
         return send(moves, lambda place: f1s.at[number, place], lambda place: f1r.at[number, place])
 
     def gather(number, field):
-        own = field.at[ta, gz]
+        own = field.at[slots[0, 0]]
         return send(
-            [(place, own, own, offset) for place, offset in enumerate(across)],
+            [(slots[cell], own, field.at[slots[cell]], (-cell[0], -cell[1], 0)) for cell in across],
             lambda place: gsend.at[number, place], lambda place: grecv.at[number, place],
         )
 
@@ -223,18 +228,7 @@
         values = parts[0]
         for k in range(1, len(parts)):
             values = jnp.where(lane % 4 == k, parts[k], values)
-        out[ta, gz] = values
-
-    def unpacked(source, t):
-        pair, odd = divmod(t, part_t)
-        values = source[pair]
-        lane = lax.broadcasted_iota(jnp.int32, values.shape, 2)
-        pieces = []
-        for z in range(part_z):
-            piece = jnp.where(lane % 4 == odd * part_z + z, values, 0.0)
-            piece = piece + pair_swap(piece, 1, 2)
-            pieces.append(piece + pair_swap(piece, 2, 2))
-        return jnp.stack(pieces, axis=1).reshape(all_z, ngy * rows2, lanes)
+        out[slots[0, 0]] = values
 
     inside = list(range(1, size_t - 1))
     ends = [0, size_t - 1]
@@ -279,8 +273,8 @@
             halved(z_pairs(slabs[2 * t] + slabs[2 * t + 1]), t, 2) for t in range(part_t)
         ]
 
-    packed(mall, to_level2([read1(m1, 2 + t, 2, size_z1) for t in range(size_t1)]))
-    mass_copies = gather(0, mall)
+    packed(m2, to_level2([read1(m1, 2 + t, 2, size_z1) for t in range(size_t1)]))
+    mass_copies = gather(0, m2)
 
     def remainder0(ts):
         for t in ts:
@@ -296,13 +290,10 @@
     remainder0((0, size_t1 - 1))
     source_copies = spread1(1, s1)
     finish(mass_copies)
-    for t in range(all_t):
-        mass = unpacked(mall, t)
-        m2[t] = mass
-        g2[t] = DAMPING / (2.0 + mass)
-    weights3 = [
-        DAMPING / (1.0 + coarse_full(m2[2 * t], m2[2 * t + 1])) for t in range(all_t // 2)
-    ]
+    for cell in stages["source"]:
+        g2[slots[cell]] = DAMPING / (2.0 + m2[slots[cell]])
+    for cell in stages["coarse"][3]:
+        m3[slots[cell]] = DAMPING / (1.0 + coarsened3(m2[slots[cell]]))
     finish(source_copies)
 
     for a, b, count in near1(2):
@@ -314,63 +305,72 @@
         remainder.append(
             read1(s1, a, b, count) + 0.5 * summed - (4.0 + read1(m1, a, b, count)) * slab
         )
-    packed(rall, to_level2(remainder))
-    finish(gather(1, rall))
-
-    for t in range(all_t):
-        source = unpacked(rall, t)
-        s2[t] = source
-        u2[t] = g2[t] * source
-
-    def sum2(field, t):
-        slab = field[t]
-        summed = field[(t - 1) % all_t] + field[(t + 1) % all_t]
-        summed = summed + shifted_z(slab, True) + shifted_z(slab, False)
-        summed = summed + rolled(slab, 1, 1) + rolled(slab, -1, 1)
-        return slab, summed + rolled(slab, 4, 2) + rolled(slab, -4, 2)
-
-    def sweep2(field, out):
-        for t in range(all_t):
-            slab, summed = sum2(field, t)
-            out[t] = KEEP * slab + g2[t] * (s2[t] + 0.25 * summed)
-
-    sweep2(u2, w2)
-    sources3 = []
-    for t in range(all_t // 2):
-        remainder = []
-        for odd in range(2):
-            slab, summed = sum2(w2, 2 * t + odd)
-            remainder.append(s2[2 * t + odd] + 0.25 * summed - (2.0 + m2[2 * t + odd]) * slab)
-        sources3.append(coarse_full(*remainder))
-
-    values = [weight * source for weight, source in zip(weights3, sources3)]
-    count = len(values)
-    for sweep_no in range(3):
-        fresh = []
-        for t in range(count):
-            slab = values[t]
-            summed = values[(t - 1) % count] + values[(t + 1) % count]
-            summed = summed + shifted_z(slab, True) + shifted_z(slab, False)
-            summed = summed + rolled(slab, 2, 1) + rolled(slab, -2, 1)
-            summed = summed + rolled(slab, 8, 2) + rolled(slab, -8, 2)
-            fresh.append(KEEP * slab + weights3[t] * (sources3[t] + 0.125 * summed))
+    packed(s2, to_level2(remainder))
+    finish(gather(1, s2))
+
+    def around2(cell):
+        t, z = cell
+        return [((t + dt) % nta, (z + dz) % ngz) for dt, dz in ((-1, 0), (1, 0), (0, -1), (0, 1))]
+
+    def sum2(field, cell):
+        slab = field[slots[cell]]
+        before_t, after_t, before_z, after_z = [
+            slab + field[slots[other]] if other in slots else slab for other in around2(cell)
+        ]
+        lane = lane_of(slab)
+        summed = jnp.where(lane % 4 >= 2, rolled(after_t, 2, 1), rolled(before_t, -2, 1))
+        summed = summed + jnp.where(lane % 2 == 1, rolled(after_z, 1, 1), rolled(before_z, -1, 1))
+        summed = summed + rolled(slab, 1, 0) + rolled(slab, -1, 0)
+        return slab, summed + rolled(slab, 4, 1) + rolled(slab, -4, 1)
+
+    def sweep2(field, out, cells):
+        for cell in cells:
+            slab, summed = sum2(field, cell)
+            at = slots[cell]
+            out[at] = KEEP * slab + g2[at] * (s2[at] + 0.25 * summed)
+
+    for cell in stages["source"]:
+        at = slots[cell]
+        u2[at] = g2[at] * s2[at]
+        w2[at] = u2[at]
+    sweep2(u2, w2, stages["swept"])
+    values = {}
+    for cell in stages["coarse"][3]:
+        slab, summed = sum2(w2, cell)
+        at = slots[cell]
+        source = coarsened3(s2[at] + 0.25 * summed - (2.0 + m2[at]) * slab)
+        s3[at] = source
+        values[cell] = m3[at] * source
+    for steps in (2, 1, 0):
+        fresh = {}
+        for cell in stages["coarse"][steps]:
+            slab = values[cell]
+            before_t, after_t, before_z, after_z = [values[other] for other in around2(cell)]
+            summed = before_t + after_t + before_z + after_z
+            summed = summed + rolled(slab, 2, 0) + rolled(slab, -2, 0)
+            summed = summed + rolled(slab, 8, 1) + rolled(slab, -8, 1)
+            fresh[cell] = KEEP * slab + m3[slots[cell]] * (s3[slots[cell]] + 0.125 * summed)
         values = fresh
-
-    for t in range(all_t):
-        w2[t] = w2[t] + refined_z(values[t // 2])
-    sweep2(w2, u2)
-    sweep2(u2, w2)
-
-    for a in range(part_t + 2):
-        at_t = lax.rem(ta * part_t + (a - 1 + all_t), all_t)
-        slabs = []
-        for b in range(part_z + 2):
-            at_z = lax.rem(gz * part_z + (b - 1 + all_z), all_z)
-            slabs.append(w2[at_t, pl.ds(at_z, 1)])
-        e2[a] = doubled(jnp.concatenate(slabs, axis=0), a)
+    for cell in stages["base"]:
+        w2[slots[cell]] = w2[slots[cell]] + refined3(values[cell])
+    for cell in stages["base"]:
+        u2[slots[cell]] = w2[slots[cell]]
+    sweep2(w2, u2, stages["first"])
+    sweep2(u2, w2, stages["last"])
+
+    def correct1(t, z):
+        piece = piece2(w2[slots[t // 2 % nta, z // 2 % ngz]], t % 2, z % 2)
+        e2[t + 1, z + 1, pl.ds(0, full // 2, stride=2), :] = piece
+        e2[t + 1, z + 1, pl.ds(1, full // 2, stride=2), :] = piece
+
+    for t in range(-1, part_t + 1):
+        for z in range(-1, part_z + 1):
+            if 0 <= t < part_t or 0 <= z < part_z:
+                correct1(t, z)
     for a, b, count in near1(1):
-        fine = refined_z(e2[a // 2])
-        write1(v1w, a, b, read1(v1b, a, b, count) + fine[b:b + count])
+        low, high = b // 2, (b + count + 1) // 2
+        fine = refined_z(e2[a // 2, pl.ds(low, high - low)])[b - 2 * low:][:count]
+        write1(v1w, a, b, read1(v1b, a, b, count) + fine)
     sweep1(v1w, v1x, 0)
     finish(send(
         around(v1x, (), (0,)), lambda place: fxs.at[place], lambda place: fxr.at[place],
@@ -423,13 +423,53 @@
     finish_sends(sent[earlier:])
 
 
-def coarse_full(even, odd):
-    summed = even + odd
-    count, rows, lanes = summed.shape
-    summed = summed.reshape(count // 2, 2, rows, lanes)
-    summed = summed[:, 0] + summed[:, 1]
-    summed = summed + pair_swap(summed, 1, 1)
-    return (summed + pair_swap(summed, 4, 2)) * 0.0625
+def lane_of(values):
+    return lax.broadcasted_iota(jnp.int32, values.shape, 1)
+
+
+def coarsened3(values):
+    for step in (1, 2, 4):
+        values = values + rolled(values, -step, 1)
+    return (values + rolled(values, -1, 0)) * 0.0625
+
+
+def refined3(values):
+    row = lax.broadcasted_iota(jnp.int32, values.shape, 0)
+    values = jnp.where((lane_of(values) % 8 == 0) & (row % 2 == 0), values, 0.0)
+    for step in (1, 2, 4):
+        values = values + rolled(values, step, 1)
+    return values + rolled(values, 1, 0)
+
+
+def piece2(values, odd_t, odd_z):
+    values = jnp.where(lane_of(values) % 4 == 2 * odd_t + odd_z, values, 0.0)
+    values = values + rolled(values, -1 if odd_z else 1, 1)
+    return values + rolled(values, -2 if odd_t else 2, 1)
+
+
+def grown(cells, steps, count_t, count_z):
+    for _ in range(steps):
+        cells = cells | {
+            ((t + dt) % count_t, (z + dz) % count_z)
+            for t, z in cells for dt, dz in ((-1, 0), (1, 0), (0, -1), (0, 1))
+        }
+    return cells
+
+
+def plan(nta, ngz):
+    sites = lambda cells, steps: grown(cells, steps, 2 * nta, 2 * ngz)
+    blocks = lambda cells: {(t // 2, z // 2) for t, z in cells}
+    inner = lambda cells: {(2 * t + a, 2 * z + b) for t, z in cells for a in (0, 1) for b in (0, 1)}
+    last = sites(inner({(0, 0)}), 1)
+    first, base = sites(last, 1), sites(last, 2)
+    coarse = [grown(blocks(base), steps, nta, ngz) for steps in range(4)]
+    swept = sites(inner(coarse[3]), 1) | base
+    ordered = lambda cells: sorted(cells, key=lambda c: ((c[0] + nta // 2) % nta, (c[1] + ngz // 2) % ngz))
+    return {
+        "last": ordered(blocks(last)), "first": ordered(blocks(first)), "base": ordered(blocks(base)),
+        "coarse": [ordered(cells) for cells in coarse], "swept": ordered(blocks(swept)),
+        "source": ordered(blocks(sites(swept, 1))),
+    }
 
 
 def per_device(sizes, right_side, mass_field):
@@ -441,17 +481,17 @@
     dma = lambda *shape: pltpu.SemaphoreType.DMA(shape)
     padded0 = vmem(size_t + 2, size_z + 2, rows, lanes)
     padded1 = vmem(size_t1 + 4, size_z1 + 4, ngy, rows1, lanes)
-    whole2 = vmem(part_t * nta, part_z * ngz, rows2 * ngy, lanes)
-    packs = vmem(nta, ngz, rows2 * ngy, lanes)
-    spreads, peers = 8 * ngy + ngy - 1, nta * ngz - 1
+    window = len(plan(nta, ngz)["source"])
+    packs = vmem(window, rows2 * ngy, lanes)
+    spreads = 8 * ngy + ngy - 1
     scratch = [
         vmem(size_t, size_z, rows, lanes), padded0, padded0, padded0, padded0, padded0,
         vmem(5, 2, size_t, size_z, 1, lanes), vmem(4, 2, size_t, size_z, 1, lanes),
         vmem(max(size_t1, part_t + 2), size_z, max(rows, ngy * rows1), lanes),
         *[padded1] * 8, vmem(part_t + 2, part_z + 2, ngy * rows1, lanes),
-        packs, packs, *[whole2] * 5,
+        *[packs] * 7,
         dma(4, 6), dma(4, 6), dma(2, spreads), dma(2, spreads), dma(8), dma(8),
-        dma(2, peers), dma(2, peers),
+        dma(2, window), dma(2, window),
         vmem(size_t, size_z, rows, lanes), vmem(size_t, size_z, rows, lanes), dma(2, size_t),
     ]
     block = jax.ShapeDtypeStruct(right_side.shape, jnp.float32)

time: 109 us -> 63.6 us (0.58)
  the two profiles are of different devices: /device:TPU:33 before, /device:TPU:8 now
where the time goes in v1:
time: 63.6 us; the launch traced here: 63.5 us
  Pallas kernels  59.2 us (93%)
  local copies, waits for them, and re-layouts  3.66 us (6%)
  between operations  0.65 us (1%)
    pallas_call x1, Pallas kernels, per_device(): pl.pallas_call(functools.partial(kernel, sizes), out_shape=(block, block)...  59.2 us
    unnamed x6, local copies, waits for them, and re-layouts  3.66 us

profile of v1, /device:TPU:8, one launch (start us, length us, event | category | flops | bytes accessed | tf_op | source)
XLA Modules:
  0.0 63.5 jit_solution(18232434583134239768)
XLA Ops:
  0.6 0.0 copy-start
  0.6 1.0 %copy-done = f32[8,8,16,128]{3,2,1,0:T(8,128)S(1)} copy-done((f32[8,8,16,128]{3,2,1,0:T(8,128)S(1)}, f32[8,8,16,128]{3,2,1,0:T(8,128)}, u32[]{:S(2)}) %copy-start) | copy-done | bytes 524312
  1.7 0.0 copy-start.1
  1.7 1.0 %copy-done.1 = f32[8,8,16,128]{3,2,1,0:T(8,128)S(1)} copy-done((f32[8,8,16,128]{3,2,1,0:T(8,128)S(1)}, f32[8,8,16,128]{3,2,1,0:T(8,128)}, u32[]{:S(2)}) %copy-start.1) | copy-done | bytes 524312
  2.7 59.2 %shard_map.41 = (f32[8,8,16,128]{3,2,1,0:T(8,128)S(1)}, f32[8,8,16,128]{3,2,1,0:T(8,128)S(1)}) custom-call(f32[8,8,16,128]{3,2,1,0:T(8,128)S(1)} %copy-done, f32[8,8,16,128]{3,2,1,0:T(8,128)S(1)} %copy-done.1), custom_call_target="tpu_custom_call" | custom-call | tf_op jit(solution)/shard_map/pallas_call | solution.py:498
  61.9 0.8 %copy.6 = f32[8,8,16,128]{3,2,1,0:T(8,128)} copy(f32[8,8,16,128]{3,2,1,0:T(8,128)S(1)} %get-tuple-element.4) | data formatting | bytes 1048576
  62.7 0.8 %copy.7 = f32[8,8,16,128]{3,2,1,0:T(8,128)} copy(f32[8,8,16,128]{3,2,1,0:T(8,128)S(1)} %get-tuple-element.5) | data formatting | bytes 1048576
Async XLA Ops:
  0.6 1.0 %copy-start = (f32[8,8,16,128]{3,2,1,0:T(8,128)S(1)}, f32[8,8,16,128]{3,2,1,0:T(8,128)}, u32[]{:S(2)}) copy-start(f32[8,8,16,128]{3,2,1,0:T(8,128)} %s_hbm.1) | copy-start | bytes 1572868
  1.7 1.0 %copy-start.1 = (f32[8,8,16,128]{3,2,1,0:T(8,128)S(1)}, f32[8,8,16,128]{3,2,1,0:T(8,128)}, u32[]{:S(2)}) copy-start(f32[8,8,16,128]{3,2,1,0:T(8,128)} %m_hbm.1) | copy-start | bytes 1572868

commit v2 on v1

--- a/solution.py
+++ b/solution.py
@@ -50,13 +50,17 @@
     slots = {cell: number for number, cell in enumerate(stages["source"])}
     ta, gz, gy = lax.axis_index("ta"), lax.axis_index("gz"), lax.axis_index("gy")
 
-    first_up = lax.min(ta, 1)
+    places = {}
+
+    def place_of(axis, at, step, count):
+        key = axis, step % count
+        if key not in places:
+            places[key] = at if key[1] == 0 else lax.rem(at + key[1], count)
+        return places[key]
 
     def device(dt, dz, dy):
         return {
-            "ta": lax.rem(ta + dt + nta, nta),
-            "gz": lax.rem(gz + dz + ngz, ngz),
-            "gy": lax.rem(gy + dy + ngy, ngy),
+            "ta": place_of("ta", ta, dt, nta), "gz": place_of("gz", gz, dz, ngz), "gy": place_of("gy", gy, dy, ngy),
         }
 
     near = [(dt, dz, dy) for dt in (-1, 0, 1) for dz in (-1, 0, 1) for dy in range(ngy)]
@@ -72,12 +76,12 @@
             pltpu.make_async_copy(s_hbm.at[pl.ds(t, 1)], s_ref.at[pl.ds(t, 1)], loaded.at[1, t]),
         ))
     met = sorted({(dt % nta, dz % ngz, dy % ngy) for dt, dz, dy in near + [(-t, -z, 0) for t, z in across]} - {(0, 0, 0)})
+    for t in [0, size_t - 1] + list(range(1, size_t - 1)):
+        for load in loads[t]:
+            load.start()
     barrier = pltpu.get_barrier_semaphore()
     for offset in met:
         pl.semaphore_signal(barrier, inc=1, device_id=device(*offset), device_id_type=MESH)
-    for t in [0, size_t - 1] + list(range(1, size_t - 1)):
-        for load in loads[t]:
-            load.start()
 
     def send(moves, sends, receives):
         copies = [
@@ -107,20 +111,16 @@
     def send0(number, moves):
         return send(moves, lambda place: f0s.at[number, place], lambda place: f0r.at[number, place])
 
-    def exchange_t(number, field):
-        moves = []
-        for up in (first_up, 1 - first_up):
-            here, there = pl.ds(1 + (size_t - 1) * up, 1), pl.ds((size_t + 1) * (1 - up), 1)
-            moves.append((up, field.at[here, inner_z], field.at[there, inner_z], (2 * up - 1, 0, 0)))
-        return send0(number, moves)
-
-    def exchange_sides(number, field, faces, halos):
-        return send0(number, [
+    def exchange(number, field, faces, halos):
+        copies = send0(number, [
+            (4, faces.at[1], halos.at[0], (0, 0, 1)),
+            (5, faces.at[0], halos.at[1], (0, 0, -1)),
             (2, field.at[inner_t, pl.ds(size_z, 1)], field.at[inner_t, pl.ds(0, 1)], (0, 1, 0)),
             (3, field.at[inner_t, pl.ds(1, 1)], field.at[inner_t, pl.ds(size_z + 1, 1)], (0, -1, 0)),
-            (4, faces.at[1], halos.at[0], (0, 0, 1)),
-            (5, faces.at[0], halos.at[1], (0, 0, -1)),
+            (1, field.at[pl.ds(size_t, 1), inner_z], field.at[pl.ds(0, 1), inner_z], (1, 0, 0)),
+            (0, field.at[pl.ds(1, 1), inner_z], field.at[pl.ds(size_t + 1, 1), inner_z], (-1, 0, 0)),
         ])
+        return copies[:4], copies[4:]
 
     def around(field, part, dys):
         own_t, own_z = pl.ds(2, size_t1), pl.ds(2, size_z1)
@@ -128,37 +128,29 @@
         def span(size, deep, up):
             return pl.ds(2 + (size - deep) * up, deep), pl.ds(2 + size - (size + deep) * up, deep)
 
+        corners, layers = [], []
+        for up in (1, 0):
+            for up_z in (1, 0):
+                here_t, there_t = span(size_t1, 1, up)
+                here_z, there_z = span(size_z1, 1, up_z)
+                corners.append((2 + 2 * up + up_z, here_t, here_z, there_t, there_z, 2 * up - 1, 2 * up_z - 1))
+        for up in (1, 0):
+            here, there = span(size_t1, 2, up)
+            layers.append((up, here, own_z, there, own_z, 2 * up - 1, 0))
+            here, there = span(size_z1, 2, up)
+            layers.append((6 + up, own_t, here, own_t, there, 0, 2 * up - 1))
         moves = []
-        for up in (first_up, 1 - first_up):
-            here, there = span(size_t1, 2, up)
-            for dy in dys:
+        for dy in reversed(dys):
+            for number, here_t, here_z, there_t, there_z, dt, dz in corners + layers:
                 moves.append((
-                    8 * dy + up, field.at[(here, own_z) + part], field.at[(there, own_z) + part],
-                    (2 * up - 1, 0, dy),
-                ))
-        for up in (1, 0):
-            here_t, there_t = span(size_t1, 1, up)
-            for up_z in (1, 0):
-                here_z, there_z = span(size_z1, 1, up_z)
-                for dy in dys:
-                    moves.append((
-                        8 * dy + 2 + 2 * up + up_z,
-                        field.at[(here_t, here_z) + part], field.at[(there_t, there_z) + part],
-                        (2 * up - 1, 2 * up_z - 1, dy),
-                    ))
-        for up in (1, 0):
-            here, there = span(size_z1, 2, up)
-            for dy in dys:
-                moves.append((
-                    8 * dy + 6 + up, field.at[(own_t, here) + part], field.at[(own_t, there) + part],
-                    (0, 2 * up - 1, dy),
+                    8 * dy + number, field.at[(here_t, here_z) + part], field.at[(there_t, there_z) + part], (dt, dz, dy),
                 ))
         return moves
 
     def spread1(number, field):
         own = field.at[pl.ds(2, size_t1), pl.ds(2, size_z1), pl.ds(gy, 1)]
-        moves = around(field, (pl.ds(gy, 1),), range(ngy))
-        moves += [(8 * ngy + dy - 1, own, own, (0, 0, dy)) for dy in range(1, ngy)]
+        moves = [(8 * ngy + dy - 1, own, own, (0, 0, dy)) for dy in range(1, ngy)]
+        moves += around(field, (pl.ds(gy, 1),), range(ngy))
         return send(moves, lambda place: f1s.at[number, place], lambda place: f1r.at[number, place])
 
     def gather(number, field):
@@ -243,8 +235,7 @@
 
     first0(ends + inside)
     pl.semaphore_wait(barrier, len(met))
-    over_t = exchange_t(0, v0a)
-    sides = exchange_sides(0, v0a, ys0.at[0], y0.at[0])
+    sides, over_t = exchange(0, v0a, ys0.at[0], y0.at[0])
     for t in range(size_t1):
         mean = halved(z_pairs(m_ref[2 * t] + m_ref[2 * t + 1]), t, 1)
         m1[t + 2, pl.ds(2, size_z1), gy] = mean
@@ -262,8 +253,7 @@
     sweep0(v0a, y0.at[0], v0b, ys0.at[1], inside)
     finish(over_t)
     sweep0(v0a, y0.at[0], v0b, ys0.at[1], ends)
-    over_t = exchange_t(1, v0b)
-    sides = exchange_sides(1, v0b, ys0.at[1], y0.at[1])
+    sides, over_t = exchange(1, v0b, ys0.at[1], y0.at[1])
     finish(mass_copies)
     for a, b, count in near1(2):
         write1(g1, a, b, DAMPING / (4.0 + read1(m1, a, b, count)))
@@ -373,7 +363,7 @@
         write1(v1w, a, b, read1(v1b, a, b, count) + fine)
     sweep1(v1w, v1x, 0)
     finish(send(
-        around(v1x, (), (0,)), lambda place: fxs.at[place], lambda place: fxr.at[place],
+        around(v1x, (), range(1)), lambda place: fxs.at[place], lambda place: fxr.at[place],
     ))
     sweep1(v1x, e1, 1)
 
@@ -396,19 +386,15 @@
                 y0[2, 0, p - 1] = y0[1, 0, p - 1] + low
                 y0[2, 1, p - 1] = y0[1, 1, p - 1] + high
 
-    corrected0((1, 2, size_t1 + 1, size_t1 + 2))
-    sweep0(v0w, y0.at[2], v0x, ys0.at[2], ends)
-    over_t = exchange_t(2, v0x)
-    corrected0(range(3, size_t1 + 1))
-    sweep0(v0w, y0.at[2], v0x, ys0.at[2], inside)
-    sides = exchange_sides(2, v0x, ys0.at[2], y0.at[3])
+    corrected0(range(1, size_t1 + 3))
+    sweep0(v0w, y0.at[2], v0x, ys0.at[2], range(size_t))
+    sides, over_t = exchange(2, v0x, ys0.at[2], y0.at[3])
     finish(sides)
     sweep0(v0x, y0.at[3], v0s, ys0.at[3], inside, sol_ref)
     finish(over_t)
     sweep0(v0x, y0.at[3], v0s, ys0.at[3], ends, sol_ref)
     earlier = len(sent)
-    over_t = exchange_t(3, v0s)
-    sides = exchange_sides(3, v0s, ys0.at[3], y0.at[4])
+    sides, over_t = exchange(3, v0s, ys0.at[3], y0.at[4])
     finish_sends(sent[:earlier])
 
     def residual(ts):
@@ -504,7 +490,7 @@
         compiler_params=pltpu.CompilerParams(
             collective_id=0, has_side_effects=True, vmem_limit_bytes=48 * 1024 * 1024
         ),
-    )(right_side, mass_field)
+    )(*[pltpu.with_memory_space_constraint(values, pltpu.HBM) for values in (right_side, mass_field)])
 
 
 def solution(mesh):

time: 63.6 us -> 60.3 us (0.948)
  the two profiles are of different devices: /device:TPU:8 before, /device:TPU:1 now
where the time goes in v2:
time: 60.3 us; the launch traced here: 60.2 us
  Pallas kernels  58 us (96%)
  local copies, waits for them, and re-layouts  1.59 us (3%)
  between operations  0.64 us (1%)
    pallas_call x1, Pallas kernels, per_device(): pl.pallas_call(functools.partial(kernel, sizes), out_shape=(block, block)...  58 us
    unnamed x2, local copies, waits for them, and re-layouts  1.59 us

profile of v2, /device:TPU:1, one launch (start us, length us, event | category | flops | bytes accessed | tf_op | source)
XLA Modules:
  0.0 60.2 jit_solution(6622406693628681965)
XLA Ops:
  0.6 58.0 %shard_map.41 = (f32[8,8,16,128]{3,2,1,0:T(8,128)S(1)}, f32[8,8,16,128]{3,2,1,0:T(8,128)S(1)}) custom-call(f32[8,8,16,128]{3,2,1,0:T(8,128)} %s_hbm.1, f32[8,8,16,128]{3,2,1,0:T(8,128)} %m_hbm.1), custom_call_target="tpu_custom_call" | custom-call | tf_op jit(solution)/shard_map/pallas_call | solution.py:484
  58.6 0.8 %copy.6 = f32[8,8,16,128]{3,2,1,0:T(8,128)} copy(f32[8,8,16,128]{3,2,1,0:T(8,128)S(1)} %get-tuple-element.4) | data formatting | bytes 1048576
  59.4 0.8 %copy.7 = f32[8,8,16,128]{3,2,1,0:T(8,128)} copy(f32[8,8,16,128]{3,2,1,0:T(8,128)S(1)} %get-tuple-element.5) | data formatting | bytes 1048576

commit v3 on v2

--- a/solution.py
+++ b/solution.py
@@ -9,11 +9,16 @@
 
 DAMPING = 0.7
 KEEP = 1.0 - DAMPING
+PAD_T, PAD_Z = 3, 2
 MESH = pl.DeviceIdType.MESH
 
 
 def rolled(values, shift, axis):
     return pltpu.roll(values, shift % values.shape[axis], axis)
+
+
+def odd_lane(values):
+    return lax.broadcasted_iota(jnp.int32, values.shape, values.ndim - 1) % 2 == 1
 
 
 def pair_swap(values, step, axis):
@@ -31,20 +36,14 @@
     return jnp.repeat(slab, 2, axis=0)
 
 
-def shifted_z(slab, forward):
-    if forward:
-        return jnp.concatenate([slab[-1:], slab[:-1]], axis=0)
-    return jnp.concatenate([slab[1:], slab[:1]], axis=0)
-
-
 def kernel(sizes, s_hbm, m_hbm, sol_ref, res_ref, *scratch):
     nta, ngz, ngy = sizes
     (g0, v0a, v0b, v0w, v0x, v0s, y0, ys0, fold,
-     s1, m1, g1, v1a, v1b, v1w, v1x, e1, e2,
+     s1, m1, g1, v1a, v1b, v1h, v1w, v1x, e1, e2,
      m2, s2, g2, u2, w2, m3, s3,
      f0s, f0r, f1s, f1r, fxs, fxr, gsend, grecv, s_ref, m_ref, loaded) = scratch
     size_t, size_z, rows, lanes = s_ref.shape
-    size_t1, size_z1, rows1 = size_t // 2, size_z // 2, rows // 2
+    size_t1, pairs1, rows1 = size_t // 2, size_z // 4, rows // 2
     part_t, part_z, rows2 = size_t // 4, size_z // 4, rows // 4
     stages = plan(nta, ngz)
     slots = {cell: number for number, cell in enumerate(stages["source"])}
@@ -122,36 +121,42 @@
         ])
         return copies[:4], copies[4:]
 
-    def around(field, part, dys):
-        own_t, own_z = pl.ds(2, size_t1), pl.ds(2, size_z1)
-
-        def span(size, deep, up):
-            return pl.ds(2 + (size - deep) * up, deep), pl.ds(2 + size - (size + deep) * up, deep)
-
-        corners, layers = [], []
+    def layers1(deep_t, deep_z, corner_t):
+        own_t, own_z = pl.ds(PAD_T, size_t1), pl.ds(PAD_Z, pairs1)
+
+        def span(pad, size, deep, up):
+            return pl.ds(pad + (size - deep) * up, deep), pl.ds(pad + size - (size + deep) * up, deep)
+
+        moves = []
         for up in (1, 0):
             for up_z in (1, 0):
-                here_t, there_t = span(size_t1, 1, up)
-                here_z, there_z = span(size_z1, 1, up_z)
-                corners.append((2 + 2 * up + up_z, here_t, here_z, there_t, there_z, 2 * up - 1, 2 * up_z - 1))
+                here_t, there_t = span(PAD_T, size_t1, corner_t, up)
+                here_z, there_z = span(PAD_Z, pairs1, 1, up_z)
+                moves.append((here_t, here_z, there_t, there_z, 2 * up - 1, 2 * up_z - 1))
         for up in (1, 0):
-            here, there = span(size_t1, 2, up)
-            layers.append((up, here, own_z, there, own_z, 2 * up - 1, 0))
-            here, there = span(size_z1, 2, up)
-            layers.append((6 + up, own_t, here, own_t, there, 0, 2 * up - 1))
-        moves = []
-        for dy in reversed(dys):
-            for number, here_t, here_z, there_t, there_z, dt, dz in corners + layers:
+            here, there = span(PAD_T, size_t1, deep_t, up)
+            moves.append((here, own_z, there, own_z, 2 * up - 1, 0))
+            here, there = span(PAD_Z, pairs1, deep_z, up)
+            moves.append((own_t, here, own_t, there, 0, 2 * up - 1))
+        return moves
+
+    def spread1(number, field):
+        part = pl.ds(gy, 1)
+        own = field.at[pl.ds(PAD_T, size_t1), pl.ds(PAD_Z, pairs1), part]
+        moves = [(8 * ngy + dy - 1, own, own, (0, 0, dy)) for dy in range(1, ngy)]
+        for dy in reversed(range(ngy)):
+            for place, (here_t, here_z, there_t, there_z, dt, dz) in enumerate(layers1(2, 1, 1)):
                 moves.append((
-                    8 * dy + number, field.at[(here_t, here_z) + part], field.at[(there_t, there_z) + part], (dt, dz, dy),
+                    8 * dy + place, field.at[here_t, here_z, part], field.at[there_t, there_z, part], (dt, dz, dy),
                 ))
-        return moves
-
-    def spread1(number, field):
-        own = field.at[pl.ds(2, size_t1), pl.ds(2, size_z1), pl.ds(gy, 1)]
-        moves = [(8 * ngy + dy - 1, own, own, (0, 0, dy)) for dy in range(1, ngy)]
-        moves += around(field, (pl.ds(gy, 1),), range(ngy))
         return send(moves, lambda place: f1s.at[number, place], lambda place: f1r.at[number, place])
+
+    def widen1(field):
+        moves = [
+            (place, field.at[here_t, here_z], field.at[there_t, there_z], (dt, dz, 0))
+            for place, (here_t, here_z, there_t, there_z, dt, dz) in enumerate(layers1(3, 2, 2))
+        ]
+        return send(moves, lambda place: fxs.at[place], lambda place: fxr.at[place])
 
     def gather(number, field):
         own = field.at[slots[0, 0]]
@@ -174,12 +179,18 @@
         summed = summed + jnp.where(row == rows - 1, halos[1, t], rolled(slab, -1, 1))
         return slab, summed + rolled(slab, 1, 2) + rolled(slab, -1, 2)
 
-    def halved(summed, place, step):
+    def folded(summed, place):
         count, high, _ = summed.shape
         view = fold.at[place, pl.ds(0, count)]
         view[...] = summed
-        summed = view[:, pl.ds(0, high // 2, stride=2), :] + view[:, pl.ds(1, high // 2, stride=2), :]
-        return (summed + pair_swap(summed, step, 2)) * 0.0625
+        return view[:, pl.ds(0, high // 2, stride=2), :] + view[:, pl.ds(1, high // 2, stride=2), :]
+
+    def to_level1(summed, place):
+        summed = folded(z_pairs(summed), place)
+        summed = summed.reshape(summed.shape[0] // 2, 2, *summed.shape[1:])
+        even, odd = summed[:, 0], summed[:, 1]
+        even, odd = even + rolled(even, -1, 2), odd + rolled(odd, 1, 2)
+        return jnp.where(odd_lane(even), odd, even) * 0.0625
 
     def doubled(slab, place):
         count, high, _ = slab.shape
@@ -191,28 +202,35 @@
     full = ngy * rows1
 
     def near1(radius):
-        for a in range(2 - radius, 2 + size_t1 + radius):
-            reach = radius - max(2 - a, a - 1 - size_t1, 0)
-            yield a, 2 - reach, size_z1 + 2 * reach
-
-    def read1(field, a, b, count):
-        return field[a, pl.ds(b, count)].reshape(count, full, lanes)
-
-    def write1(field, a, b, slab):
-        field[a, pl.ds(b, slab.shape[0])] = slab.reshape(slab.shape[0], ngy, rows1, lanes)
-
-    def sum1(field, a, b, count):
-        slab = read1(field, a, b, count)
-        summed = read1(field, a - 1, b, count) + read1(field, a + 1, b, count)
-        summed = summed + read1(field, a, b - 1, count) + read1(field, a, b + 1, count)
+        for t in range(-radius, size_t1 + radius):
+            reach = (radius - max(-t, t - size_t1 + 1, 0) + 1) // 2
+            yield t, -reach, pairs1 + 2 * reach
+
+    def read1(field, t, z, count):
+        return field[PAD_T + t, pl.ds(PAD_Z + z, count)].reshape(count, full, lanes)
+
+    def write1(field, t, z, slab):
+        field[PAD_T + t, pl.ds(PAD_Z + z, slab.shape[0])] = slab.reshape(slab.shape[0], ngy, rows1, lanes)
+
+    def sum1(field, t, z, count, held):
+        slab = read1(field, t, z, count)
+        summed = read1(field, t - 1, z, count) + read1(field, t + 1, z, count)
+        if held[t][0] < z:
+            before, after = read1(field, t, z - 1, count), read1(field, t, z + 1, count)
+        else:
+            before = jnp.concatenate([slab[:1], slab[:-1]], axis=0)
+            after = jnp.concatenate([slab[1:], slab[-1:]], axis=0)
+        summed = summed + jnp.where(odd_lane(slab), rolled(slab + after, 1, 2), rolled(slab + before, -1, 2))
         summed = summed + rolled(slab, 1, 1) + rolled(slab, -1, 1)
         return slab, summed + rolled(slab, 2, 2) + rolled(slab, -2, 2)
 
+    held1 = [{t: (z, count) for t, z, count in near1(radius)} for radius in range(4)]
+
     def sweep1(field, out, radius):
-        for a, b, count in near1(radius):
-            slab, summed = sum1(field, a, b, count)
-            fresh = KEEP * slab + read1(g1, a, b, count) * (read1(s1, a, b, count) + 0.5 * summed)
-            write1(out, a, b, fresh)
+        for t, z, count in near1(radius):
+            slab, summed = sum1(field, t, z, count, held1[radius + 1])
+            fresh = KEEP * slab + read1(g1, t, z, count) * (read1(s1, t, z, count) + 0.5 * summed)
+            write1(out, t, z, fresh)
 
     def packed(out, slabs):
         parts = [slab[z] for slab in slabs for z in range(part_z)]
@@ -237,8 +255,7 @@
     pl.semaphore_wait(barrier, len(met))
     sides, over_t = exchange(0, v0a, ys0.at[0], y0.at[0])
     for t in range(size_t1):
-        mean = halved(z_pairs(m_ref[2 * t] + m_ref[2 * t + 1]), t, 1)
-        m1[t + 2, pl.ds(2, size_z1), gy] = mean
+        m1[PAD_T + t, pl.ds(PAD_Z, pairs1), gy] = to_level1(m_ref[2 * t] + m_ref[2 * t + 1], t)
     mass_copies = spread1(0, m1)
 
     def sweep0(field, halos, out, faces, ts, also=None):
@@ -259,11 +276,14 @@
         write1(g1, a, b, DAMPING / (4.0 + read1(m1, a, b, count)))
 
     def to_level2(slabs):
-        return [
-            halved(z_pairs(slabs[2 * t] + slabs[2 * t + 1]), t, 2) for t in range(part_t)
-        ]
-
-    packed(m2, to_level2([read1(m1, 2 + t, 2, size_z1) for t in range(size_t1)]))
+        out = []
+        for t in range(part_t):
+            summed = folded(slabs[2 * t] + slabs[2 * t + 1], t)
+            summed = summed + pair_swap(summed, 1, 2)
+            out.append((summed + pair_swap(summed, 2, 2)) * 0.0625)
+        return out
+
+    packed(m2, to_level2([read1(m1, t, 0, pairs1) for t in range(size_t1)]))
     mass_copies = gather(0, m2)
 
     def remainder0(ts):
@@ -272,7 +292,7 @@
             for odd in range(2):
                 slab, summed = sum0(v0b, y0.at[1], 2 * t + odd)
                 remainder.append(s_ref[2 * t + odd] + summed - (8.0 + m_ref[2 * t + odd]) * slab)
-            s1[t + 2, pl.ds(2, size_z1), gy] = halved(z_pairs(remainder[0] + remainder[1]), t, 1)
+            s1[PAD_T + t, pl.ds(PAD_Z, pairs1), gy] = to_level1(remainder[0] + remainder[1], t)
 
     finish(sides)
     remainder0(range(1, size_t1 - 1))
@@ -291,12 +311,15 @@
     sweep1(v1a, v1b, 1)
     remainder = []
     for a, b, count in near1(0):
-        slab, summed = sum1(v1b, a, b, count)
+        slab, summed = sum1(v1b, a, b, count, held1[1])
+        write1(v1h, a, b, slab)
         remainder.append(
             read1(s1, a, b, count) + 0.5 * summed - (4.0 + read1(m1, a, b, count)) * slab
         )
     packed(s2, to_level2(remainder))
-    finish(gather(1, s2))
+    source_copies = gather(1, s2)
+    wide_copies = widen1(v1h)
+    finish(source_copies)
 
     def around2(cell):
         t, z = cell
@@ -350,43 +373,46 @@
 
     def correct1(t, z):
         piece = piece2(w2[slots[t // 2 % nta, z // 2 % ngz]], t % 2, z % 2)
-        e2[t + 1, z + 1, pl.ds(0, full // 2, stride=2), :] = piece
-        e2[t + 1, z + 1, pl.ds(1, full // 2, stride=2), :] = piece
-
-    for t in range(-1, part_t + 1):
-        for z in range(-1, part_z + 1):
-            if 0 <= t < part_t or 0 <= z < part_z:
+        e2[t + 2, z + 2, pl.ds(0, full // 2, stride=2), :] = piece
+        e2[t + 2, z + 2, pl.ds(1, full // 2, stride=2), :] = piece
+
+    for t in range(-2, part_t + 2):
+        for z in range(-2, part_z + 2):
+            if max(-t, t - part_t + 1, 0) + max(-z, z - part_z + 1, 0) <= 2:
                 correct1(t, z)
-    for a, b, count in near1(1):
-        low, high = b // 2, (b + count + 1) // 2
-        fine = refined_z(e2[a // 2, pl.ds(low, high - low)])[b - 2 * low:][:count]
-        write1(v1w, a, b, read1(v1b, a, b, count) + fine)
-    sweep1(v1w, v1x, 0)
-    finish(send(
-        around(v1x, (), range(1)), lambda place: fxs.at[place], lambda place: fxr.at[place],
-    ))
+    finish(wide_copies)
+    for t, z, count in near1(3):
+        write1(v1w, t, z, read1(v1h, t, z, count) + e2[t // 2 + 2, pl.ds(z + 2, count)])
+    sweep1(v1w, v1x, 2)
     sweep1(v1x, e1, 1)
 
     under = lax.rem(gy + ngy - 1, ngy)
     over = lax.rem(gy + 1, ngy)
+
+    def split1(slab):
+        even = jnp.where(odd_lane(slab), rolled(slab, 1, 2), slab)
+        odd = jnp.where(odd_lane(slab), slab, rolled(slab, -1, 2))
+        return jnp.stack([even, odd], axis=1).reshape(2 * slab.shape[0], *slab.shape[1:])
+
     def corrected0(layers):
-        for at_t in layers:
-            own = [p for p in (2 * at_t - 3, 2 * at_t - 2) if 1 <= p <= size_t]
+        for t in layers:
+            own = [p for p in (2 * t + 1, 2 * t + 2) if 1 <= p <= size_t]
             if not own:
-                p = 0 if at_t == 1 else size_t + 1
-                fine = refined_z(doubled(e1[at_t, pl.ds(2, size_z1), gy], 0))
+                p = 0 if t < 0 else size_t + 1
+                fine = refined_z(doubled(split1(e1[PAD_T + t, pl.ds(PAD_Z, pairs1), gy]), 0))
                 v0w[p, inner_z] = v0b[p, inner_z] + fine
                 continue
-            fine = refined_z(doubled(e1[at_t, pl.ds(1, size_z1 + 2), gy], at_t % 4))
+            fine = split1(e1[PAD_T + t, pl.ds(PAD_Z - 1, pairs1 + 2), gy])
+            fine = refined_z(doubled(fine[1:-1], t % 4))
             fine = fine[1:1 + size_z + 2]
-            low = refined_z(e1[at_t, pl.ds(2, size_z1), under, pl.ds(rows1 - 1, 1)])
-            high = refined_z(e1[at_t, pl.ds(2, size_z1), over, pl.ds(0, 1)])
+            low = refined_z(split1(e1[PAD_T + t, pl.ds(PAD_Z, pairs1), under, pl.ds(rows1 - 1, 1)]))
+            high = refined_z(split1(e1[PAD_T + t, pl.ds(PAD_Z, pairs1), over, pl.ds(0, 1)]))
             for p in own:
                 v0w[p] = v0b[p] + fine
                 y0[2, 0, p - 1] = y0[1, 0, p - 1] + low
                 y0[2, 1, p - 1] = y0[1, 1, p - 1] + high
 
-    corrected0(range(1, size_t1 + 3))
+    corrected0(range(-1, size_t1 + 1))
     sweep0(v0w, y0.at[2], v0x, ys0.at[2], range(size_t))
     sides, over_t = exchange(2, v0x, ys0.at[2], y0.at[3])
     finish(sides)
@@ -446,7 +472,7 @@
     sites = lambda cells, steps: grown(cells, steps, 2 * nta, 2 * ngz)
     blocks = lambda cells: {(t // 2, z // 2) for t, z in cells}
     inner = lambda cells: {(2 * t + a, 2 * z + b) for t, z in cells for a in (0, 1) for b in (0, 1)}
-    last = sites(inner({(0, 0)}), 1)
+    last = sites(inner({(0, 0)}), 2)
     first, base = sites(last, 1), sites(last, 2)
     coarse = [grown(blocks(base), steps, nta, ngz) for steps in range(4)]
     swept = sites(inner(coarse[3]), 1) | base
@@ -461,12 +487,12 @@
 def per_device(sizes, right_side, mass_field):
     nta, ngz, ngy = sizes
     size_t, size_z, rows, lanes = right_side.shape
-    size_t1, size_z1, rows1 = size_t // 2, size_z // 2, rows // 2
+    size_t1, pairs1, rows1 = size_t // 2, size_z // 4, rows // 2
     part_t, part_z, rows2 = size_t // 4, size_z // 4, rows // 4
     vmem = lambda *shape: pltpu.VMEM(shape, jnp.float32)
     dma = lambda *shape: pltpu.SemaphoreType.DMA(shape)
     padded0 = vmem(size_t + 2, size_z + 2, rows, lanes)
-    padded1 = vmem(size_t1 + 4, size_z1 + 4, ngy, rows1, lanes)
+    padded1 = vmem(size_t1 + 2 * PAD_T, pairs1 + 2 * PAD_Z, ngy, rows1, lanes)
     window = len(plan(nta, ngz)["source"])
     packs = vmem(window, rows2 * ngy, lanes)
     spreads = 8 * ngy + ngy - 1
@@ -474,7 +500,7 @@
         vmem(size_t, size_z, rows, lanes), padded0, padded0, padded0, padded0, padded0,
         vmem(5, 2, size_t, size_z, 1, lanes), vmem(4, 2, size_t, size_z, 1, lanes),
         vmem(max(size_t1, part_t + 2), size_z, max(rows, ngy * rows1), lanes),
-        *[padded1] * 8, vmem(part_t + 2, part_z + 2, ngy * rows1, lanes),
+        *[padded1] * 9, vmem(part_t + 4, part_z + 4, ngy * rows1, lanes),
         *[packs] * 7,
         dma(4, 6), dma(4, 6), dma(2, spreads), dma(2, spreads), dma(8), dma(8),
         dma(2, window), dma(2, window),

time: 60.3 us -> 59.7 us (0.990)
  Pallas kernels: 58 us -> 57.3 us
    pallas_call x1, Pallas kernels: 58 us -> 57.3 us  [per_device(): pl.pallas_call(functools.partial(kernel, sizes), out_shape=(block, block)...]
where the time goes in v3:
time: 59.7 us; the launch traced here: 59.6 us
  Pallas kernels  57.3 us (96%)
  local copies, waits for them, and re-layouts  1.59 us (3%)
  between operations  0.64 us (1%)
    pallas_call x1, Pallas kernels, per_device(): pl.pallas_call(functools.partial(kernel, sizes), out_shape=(block, block)...  57.3 us
    unnamed x2, local copies, waits for them, and re-layouts  1.59 us

profile of v3, /device:TPU:1, one launch (start us, length us, event | category | flops | bytes accessed | tf_op | source)
XLA Modules:
  0.0 59.6 jit_solution(1007660977603711380)
XLA Ops:
  0.6 57.3 %shard_map.41 = (f32[8,8,16,128]{3,2,1,0:T(8,128)S(1)}, f32[8,8,16,128]{3,2,1,0:T(8,128)S(1)}) custom-call(f32[8,8,16,128]{3,2,1,0:T(8,128)} %s_hbm.1, f32[8,8,16,128]{3,2,1,0:T(8,128)} %m_hbm.1), custom_call_target="tpu_custom_call" | custom-call | tf_op jit(solution)/shard_map/pallas_call | solution.py:510
  58.0 0.8 %copy.6 = f32[8,8,16,128]{3,2,1,0:T(8,128)} copy(f32[8,8,16,128]{3,2,1,0:T(8,128)S(1)} %get-tuple-element.4) | data formatting | bytes 1048576
  58.8 0.8 %copy.7 = f32[8,8,16,128]{3,2,1,0:T(8,128)} copy(f32[8,8,16,128]{3,2,1,0:T(8,128)S(1)} %get-tuple-element.5) | data formatting | bytes 1048576

commit v4 on v3

--- a/solution.py
+++ b/solution.py
@@ -40,13 +40,14 @@
     nta, ngz, ngy = sizes
     (g0, v0a, v0b, v0w, v0x, v0s, y0, ys0, fold,
      s1, m1, g1, v1a, v1b, v1h, v1w, v1x, e1, e2,
-     m2, s2, g2, u2, w2, m3, s3,
+     m2, s2, g2, u2, w2, m3, s3, u3, w3,
      f0s, f0r, f1s, f1r, fxs, fxr, gsend, grecv, s_ref, m_ref, loaded) = scratch
     size_t, size_z, rows, lanes = s_ref.shape
     size_t1, pairs1, rows1 = size_t // 2, size_z // 4, rows // 2
     part_t, part_z, rows2 = size_t // 4, size_z // 4, rows // 4
     stages = plan(nta, ngz)
     slots = {cell: number for number, cell in enumerate(stages["source"])}
+    slots3 = {cell: number for number, cell in enumerate(stages["coarse"][3])}
     ta, gz, gy = lax.axis_index("ta"), lax.axis_index("gz"), lax.axis_index("gy")
 
     places = {}
@@ -299,11 +300,17 @@
     finish(over_t)
     remainder0((0, size_t1 - 1))
     source_copies = spread1(1, s1)
+    def take(field, places, cells):
+        return jnp.stack([field[places[cell]] for cell in cells])
+
+    def put3(field, cells, values):
+        field[pl.ds(slots3[cells[0]], len(cells))] = values
+
     finish(mass_copies)
     for cell in stages["source"]:
         g2[slots[cell]] = DAMPING / (2.0 + m2[slots[cell]])
-    for cell in stages["coarse"][3]:
-        m3[slots[cell]] = DAMPING / (1.0 + coarsened3(m2[slots[cell]]))
+    for cells in batches(stages["coarse"][3], 24):
+        put3(m3, cells, DAMPING / (1.0 + coarsened3(take(m2, slots, cells))))
     finish(source_copies)
 
     for a, b, count in near1(2):
@@ -330,7 +337,7 @@
         before_t, after_t, before_z, after_z = [
             slab + field[slots[other]] if other in slots else slab for other in around2(cell)
         ]
-        lane = lane_of(slab)
+        lane = place_in(slab, 1)
         summed = jnp.where(lane % 4 >= 2, rolled(after_t, 2, 1), rolled(before_t, -2, 1))
         summed = summed + jnp.where(lane % 2 == 1, rolled(after_z, 1, 1), rolled(before_z, -1, 1))
         summed = summed + rolled(slab, 1, 0) + rolled(slab, -1, 0)
@@ -347,25 +354,31 @@
         u2[at] = g2[at] * s2[at]
         w2[at] = u2[at]
     sweep2(u2, w2, stages["swept"])
-    values = {}
     for cell in stages["coarse"][3]:
         slab, summed = sum2(w2, cell)
         at = slots[cell]
-        source = coarsened3(s2[at] + 0.25 * summed - (2.0 + m2[at]) * slab)
-        s3[at] = source
-        values[cell] = m3[at] * source
+        s3[slots3[cell]] = s2[at] + 0.25 * summed - (2.0 + m2[at]) * slab
+    for cells in batches(stages["coarse"][3], 24):
+        source = coarsened3(take(s3, slots3, cells))
+        put3(s3, cells, source)
+        put3(u3, cells, take(m3, slots3, cells) * source)
+    old, new = u3, w3
     for steps in (2, 1, 0):
-        fresh = {}
-        for cell in stages["coarse"][steps]:
-            slab = values[cell]
-            before_t, after_t, before_z, after_z = [values[other] for other in around2(cell)]
-            summed = before_t + after_t + before_z + after_z
-            summed = summed + rolled(slab, 2, 0) + rolled(slab, -2, 0)
-            summed = summed + rolled(slab, 8, 1) + rolled(slab, -8, 1)
-            fresh[cell] = KEEP * slab + m3[slots[cell]] * (s3[slots[cell]] + 0.125 * summed)
-        values = fresh
-    for cell in stages["base"]:
-        w2[slots[cell]] = w2[slots[cell]] + refined3(values[cell])
+        for cells in batches(stages["coarse"][steps], 13):
+            slab = take(old, slots3, cells)
+            near3 = list(zip(*[around2(cell) for cell in cells]))
+            summed = take(old, slots3, near3[0]) + take(old, slots3, near3[1])
+            summed = summed + take(old, slots3, near3[2]) + take(old, slots3, near3[3])
+            summed = summed + rolled(slab, 2, 1) + rolled(slab, -2, 1)
+            summed = summed + rolled(slab, 8, 2) + rolled(slab, -8, 2)
+            fresh = KEEP * slab + take(m3, slots3, cells) * (take(s3, slots3, cells) + 0.125 * summed)
+            for number, cell in enumerate(cells):
+                new[slots3[cell]] = fresh[number]
+        old, new = new, old
+    for cells in batches(stages["base"], 24):
+        fine = refined3(take(old, slots3, cells))
+        for number, cell in enumerate(cells):
+            w2[slots[cell]] = w2[slots[cell]] + fine[number]
     for cell in stages["base"]:
         u2[slots[cell]] = w2[slots[cell]]
     sweep2(w2, u2, stages["first"])
@@ -435,28 +448,35 @@
     finish_sends(sent[earlier:])
 
 
-def lane_of(values):
-    return lax.broadcasted_iota(jnp.int32, values.shape, 1)
+def place_in(values, axis):
+    return lax.broadcasted_iota(jnp.int32, values.shape, axis)
 
 
 def coarsened3(values):
     for step in (1, 2, 4):
-        values = values + rolled(values, -step, 1)
-    return (values + rolled(values, -1, 0)) * 0.0625
+        values = values + rolled(values, -step, 2)
+    return (values + rolled(values, -1, 1)) * 0.0625
 
 
 def refined3(values):
-    row = lax.broadcasted_iota(jnp.int32, values.shape, 0)
-    values = jnp.where((lane_of(values) % 8 == 0) & (row % 2 == 0), values, 0.0)
+    corner = (place_in(values, 2) % 8 == 0) & (place_in(values, 1) % 2 == 0)
+    values = jnp.where(corner, values, 0.0)
+    values = values + rolled(values, 1, 1)
     for step in (1, 2, 4):
-        values = values + rolled(values, step, 1)
-    return values + rolled(values, 1, 0)
+        values = values + rolled(values, step, 2)
+    return values
 
 
 def piece2(values, odd_t, odd_z):
-    values = jnp.where(lane_of(values) % 4 == 2 * odd_t + odd_z, values, 0.0)
+    values = jnp.where(place_in(values, 1) % 4 == 2 * odd_t + odd_z, values, 0.0)
     values = values + rolled(values, -1 if odd_z else 1, 1)
     return values + rolled(values, -2 if odd_t else 2, 1)
+
+
+def batches(cells, most):
+    count = -(-len(cells) // most)
+    size = -(-len(cells) // count)
+    return [cells[at:at + size] for at in range(0, len(cells), size)]
 
 
 def grown(cells, steps, count_t, count_z):
@@ -495,13 +515,14 @@
     padded1 = vmem(size_t1 + 2 * PAD_T, pairs1 + 2 * PAD_Z, ngy, rows1, lanes)
     window = len(plan(nta, ngz)["source"])
     packs = vmem(window, rows2 * ngy, lanes)
+    packs3 = vmem(len(plan(nta, ngz)["coarse"][3]), rows2 * ngy, lanes)
     spreads = 8 * ngy + ngy - 1
     scratch = [
         vmem(size_t, size_z, rows, lanes), padded0, padded0, padded0, padded0, padded0,
         vmem(5, 2, size_t, size_z, 1, lanes), vmem(4, 2, size_t, size_z, 1, lanes),
         vmem(max(size_t1, part_t + 2), size_z, max(rows, ngy * rows1), lanes),
         *[padded1] * 9, vmem(part_t + 4, part_z + 4, ngy * rows1, lanes),
-        *[packs] * 7,
+        *[packs] * 5, *[packs3] * 4,
         dma(4, 6), dma(4, 6), dma(2, spreads), dma(2, spreads), dma(8), dma(8),
         dma(2, window), dma(2, window),
         vmem(size_t, size_z, rows, lanes), vmem(size_t, size_z, rows, lanes), dma(2, size_t),

time: 59.7 us -> 53.6 us (0.90)
  Pallas kernels: 57.3 us -> 51.2 us
    pallas_call x1, Pallas kernels: 57.3 us -> 51.2 us  [per_device(): pl.pallas_call(functools.partial(kernel, sizes), out_shape=(block, block)...]
where the time goes in v4:
time: 53.6 us; the launch traced here: 53.4 us
  Pallas kernels  51.2 us (96%)
  local copies, waits for them, and re-layouts  1.59 us (3%)
  between operations  0.64 us (1%)
    pallas_call x1, Pallas kernels, per_device(): pl.pallas_call(functools.partial(kernel, sizes), out_shape=(block, block)...  51.2 us
    unnamed x2, local copies, waits for them, and re-layouts  1.59 us

profile of v4, /device:TPU:1, one launch (start us, length us, event | category | flops | bytes accessed | tf_op | source)
XLA Modules:
  0.0 53.4 jit_solution(16084309269022915259)
XLA Ops:
  0.6 51.2 %shard_map.41 = (f32[8,8,16,128]{3,2,1,0:T(8,128)S(1)}, f32[8,8,16,128]{3,2,1,0:T(8,128)S(1)}) custom-call(f32[8,8,16,128]{3,2,1,0:T(8,128)} %s_hbm.1, f32[8,8,16,128]{3,2,1,0:T(8,128)} %m_hbm.1), custom_call_target="tpu_custom_call" | custom-call | tf_op jit(solution)/shard_map/pallas_call | solution.py:531
  51.8 0.8 %copy.6 = f32[8,8,16,128]{3,2,1,0:T(8,128)} copy(f32[8,8,16,128]{3,2,1,0:T(8,128)S(1)} %get-tuple-element.4) | data formatting | bytes 1048576
  52.6 0.8 %copy.7 = f32[8,8,16,128]{3,2,1,0:T(8,128)} copy(f32[8,8,16,128]{3,2,1,0:T(8,128)S(1)} %get-tuple-element.5) | data formatting | bytes 1048576

commit v5 on v4

--- a/solution.py
+++ b/solution.py
@@ -9,7 +9,7 @@
 
 DAMPING = 0.7
 KEEP = 1.0 - DAMPING
-PAD_T, PAD_Z = 3, 2
+PAD0, PAD_T, PAD_Z = 2, 3, 2
 MESH = pl.DeviceIdType.MESH
 
 
@@ -38,10 +38,10 @@
 
 def kernel(sizes, s_hbm, m_hbm, sol_ref, res_ref, *scratch):
     nta, ngz, ngy = sizes
-    (g0, v0a, v0b, v0w, v0x, v0s, y0, ys0, fold,
+    (g0, v0a, v0b, v0w, v0x, v0s, y0, ys0, y2, ys2, yg, ysg, fold,
      s1, m1, g1, v1a, v1b, v1h, v1w, v1x, e1, e2,
      m2, s2, g2, u2, w2, m3, s3, u3, w3,
-     f0s, f0r, f1s, f1r, fxs, fxr, gsend, grecv, s_ref, m_ref, loaded) = scratch
+     f0s, f0r, fhs, fhr, f1s, f1r, fxs, fxr, gsend, grecv, s_ref, m_ref, loaded) = scratch
     size_t, size_z, rows, lanes = s_ref.shape
     size_t1, pairs1, rows1 = size_t // 2, size_z // 4, rows // 2
     part_t, part_z, rows2 = size_t // 4, size_z // 4, rows // 4
@@ -106,21 +106,59 @@
         for copy in copies:
             copy.wait_send()
 
-    inner_t, inner_z = pl.ds(1, size_t), pl.ds(1, size_z)
-
-    def send0(number, moves):
-        return send(moves, lambda place: f0s.at[number, place], lambda place: f0r.at[number, place])
-
-    def exchange(number, field, faces, halos):
-        copies = send0(number, [
-            (4, faces.at[1], halos.at[0], (0, 0, 1)),
-            (5, faces.at[0], halos.at[1], (0, 0, -1)),
-            (2, field.at[inner_t, pl.ds(size_z, 1)], field.at[inner_t, pl.ds(0, 1)], (0, 1, 0)),
-            (3, field.at[inner_t, pl.ds(1, 1)], field.at[inner_t, pl.ds(size_z + 1, 1)], (0, -1, 0)),
-            (1, field.at[pl.ds(size_t, 1), inner_z], field.at[pl.ds(0, 1), inner_z], (1, 0, 0)),
-            (0, field.at[pl.ds(1, 1), inner_z], field.at[pl.ds(size_t + 1, 1), inner_z], (-1, 0, 0)),
-        ])
+    inner_t, inner_z = pl.ds(PAD0, size_t), pl.ds(PAD0, size_z)
+
+    def faces0(field, depth):
+        one = lambda at: pl.ds(PAD0 + at, 1)
+        return [
+            (field.at[inner_t, one(size_z - depth)], field.at[inner_t, one(-depth)], (0, 1, 0)),
+            (field.at[inner_t, one(depth - 1)], field.at[inner_t, one(size_z - 1 + depth)], (0, -1, 0)),
+            (field.at[one(size_t - depth), inner_z], field.at[one(-depth), inner_z], (1, 0, 0)),
+            (field.at[one(depth - 1), inner_z], field.at[one(size_t - 1 + depth), inner_z], (-1, 0, 0)),
+        ]
+
+    own_t, own_z = pl.ds(1, size_t), pl.ds(1, size_z)
+
+    def exchange(number, field):
+        faces, halos = ys0.at[number], y0.at[(0, 1, 4)[number]]
+        moves = [
+            (faces.at[1], halos.at[0, own_t, own_z], (0, 0, 1)), (faces.at[0], halos.at[1, own_t, own_z], (0, 0, -1)),
+        ] + faces0(field, 1)
+        copies = send(
+            [(place, *move) for place, move in enumerate(moves)],
+            lambda place: f0s.at[number, place], lambda place: f0r.at[number, place],
+        )
         return copies[:4], copies[4:]
+
+    def behind():
+        one = lambda at: pl.ds(at, 1)
+        moves = [
+            (ys2.at[1], y2.at[0, 0], (0, 0, 1)), (ys2.at[0], y2.at[0, 1], (0, 0, -1)),
+            (ysg.at[1], yg.at[0], (0, 0, 1)), (ysg.at[0], yg.at[1], (0, 0, -1)),
+        ]
+        for up_t in (1, 0):
+            for up_z in (1, 0):
+                moves.append((
+                    v0b.at[one(PAD0 + (size_t - 1) * up_t), one(PAD0 + (size_z - 1) * up_z)],
+                    v0b.at[one(PAD0 - 1 + (size_t + 1) * (1 - up_t)), one(PAD0 - 1 + (size_z + 1) * (1 - up_z))],
+                    (2 * up_t - 1, 2 * up_z - 1, 0),
+                ))
+        for up_y in (1, 0):
+            faces, halos = ys0.at[1, up_y], y0.at[1, 1 - up_y]
+            for up in (1, 0):
+                moves.append((
+                    faces.at[one((size_t - 1) * up)], halos.at[one((size_t + 1) * (1 - up)), own_z],
+                    (2 * up - 1, 0, 2 * up_y - 1),
+                ))
+                moves.append((
+                    faces.at[:, one((size_z - 1) * up)], halos.at[own_t, one((size_z + 1) * (1 - up))],
+                    (0, 2 * up - 1, 2 * up_y - 1),
+                ))
+        moves += faces0(v0b, 2) + faces0(g0, 1)
+        return send(
+            [(place, *move) for place, move in enumerate(moves)],
+            lambda place: fhs.at[place], lambda place: fhr.at[place],
+        )
 
     def layers1(deep_t, deep_z, corner_t):
         own_t, own_z = pl.ds(PAD_T, size_t1), pl.ds(PAD_Z, pairs1)
@@ -146,7 +184,7 @@
         own = field.at[pl.ds(PAD_T, size_t1), pl.ds(PAD_Z, pairs1), part]
         moves = [(8 * ngy + dy - 1, own, own, (0, 0, dy)) for dy in range(1, ngy)]
         for dy in reversed(range(ngy)):
-            for place, (here_t, here_z, there_t, there_z, dt, dz) in enumerate(layers1(2, 1, 1)):
+            for place, (here_t, here_z, there_t, there_z, dt, dz) in enumerate(layers1(2, 1, 2)):
                 moves.append((
                     8 * dy + place, field.at[here_t, here_z, part], field.at[there_t, there_z, part], (dt, dz, dy),
                 ))
@@ -155,8 +193,17 @@
     def widen1(field):
         moves = [
             (place, field.at[here_t, here_z], field.at[there_t, there_z], (dt, dz, 0))
-            for place, (here_t, here_z, there_t, there_z, dt, dz) in enumerate(layers1(3, 2, 2))
+            for place, (here_t, here_z, there_t, there_z, dt, dz) in enumerate(layers1(3, 2, 3))
         ]
+        one = lambda at: pl.ds(at, 1)
+        for up in (1, 0):
+            for up_z in (1, 0):
+                moves.append((
+                    len(moves),
+                    field.at[one(PAD_T + (size_t1 - 1) * up), one(PAD_Z + 1 + (pairs1 - 3) * up_z)],
+                    field.at[one(PAD_T - 1 + (size_t1 + 1) * (1 - up)), one(PAD_Z - 2 + (pairs1 + 3) * (1 - up_z))],
+                    (2 * up - 1, 2 * up_z - 1, 0),
+                ))
         return send(moves, lambda place: fxs.at[place], lambda place: fxr.at[place])
 
     def gather(number, field):
@@ -167,17 +214,18 @@
         )
 
     def put(field, faces, t, slab):
-        field[t + 1, pl.ds(1, size_z)] = slab
+        field[PAD0 + t, inner_z] = slab
         faces[0, t] = slab[:, :1]
         faces[1, t] = slab[:, rows - 1:]
 
-    def sum0(field, halos, t):
-        slab = field[t + 1, pl.ds(1, size_z)]
+    def sum0(field, halos, t, reach=0):
+        count = size_z + 2 * reach
+        at = lambda dt, dz: field[PAD0 + t + dt, pl.ds(PAD0 - reach + dz, count)]
+        slab, out = at(0, 0), pl.ds(1 - reach, count)
         row = lax.broadcasted_iota(jnp.int32, slab.shape, 1)
-        summed = field[t, pl.ds(1, size_z)] + field[t + 2, pl.ds(1, size_z)]
-        summed = summed + field[t + 1, pl.ds(0, size_z)] + field[t + 1, pl.ds(2, size_z)]
-        summed = summed + jnp.where(row == 0, halos[0, t], rolled(slab, 1, 1))
-        summed = summed + jnp.where(row == rows - 1, halos[1, t], rolled(slab, -1, 1))
+        summed = at(-1, 0) + at(1, 0) + at(0, -1) + at(0, 1)
+        summed = summed + jnp.where(row == 0, halos[0, 1 + t, out], rolled(slab, 1, 1))
+        summed = summed + jnp.where(row == rows - 1, halos[1, 1 + t, out], rolled(slab, -1, 1))
         return slab, summed + rolled(slab, 1, 2) + rolled(slab, -1, 2)
 
     def folded(summed, place):
@@ -202,9 +250,10 @@
 
     full = ngy * rows1
 
-    def near1(radius):
-        for t in range(-radius, size_t1 + radius):
-            reach = (radius - max(-t, t - size_t1 + 1, 0) + 1) // 2
+    def area1(*reaches):
+        far = len(reaches) - 1
+        for t in range(-far, size_t1 + far):
+            reach = reaches[max(-t, t - size_t1 + 1, 0)]
             yield t, -reach, pairs1 + 2 * reach
 
     def read1(field, t, z, count):
@@ -225,11 +274,10 @@
         summed = summed + rolled(slab, 1, 1) + rolled(slab, -1, 1)
         return slab, summed + rolled(slab, 2, 2) + rolled(slab, -2, 2)
 
-    held1 = [{t: (z, count) for t, z, count in near1(radius)} for radius in range(4)]
-
-    def sweep1(field, out, radius):
-        for t, z, count in near1(radius):
-            slab, summed = sum1(field, t, z, count, held1[radius + 1])
+    def sweep1(field, out, area, held):
+        held = {t: (z, count) for t, z, count in area1(*held)}
+        for t, z, count in area1(*area):
+            slab, summed = sum1(field, t, z, count, held)
             fresh = KEEP * slab + read1(g1, t, z, count) * (read1(s1, t, z, count) + 0.5 * summed)
             write1(out, t, z, fresh)
 
@@ -249,12 +297,12 @@
             for load in loads[t]:
                 load.wait()
             weight = DAMPING / (8.0 + m_ref[t])
-            g0[t] = weight
+            put(g0, ysg, t, weight)
             put(v0a, ys0.at[0], t, weight * s_ref[t])
 
     first0(ends + inside)
     pl.semaphore_wait(barrier, len(met))
-    sides, over_t = exchange(0, v0a, ys0.at[0], y0.at[0])
+    sides, over_t = exchange(0, v0a)
     for t in range(size_t1):
         m1[PAD_T + t, pl.ds(PAD_Z, pairs1), gy] = to_level1(m_ref[2 * t] + m_ref[2 * t + 1], t)
     mass_copies = spread1(0, m1)
@@ -262,7 +310,7 @@
     def sweep0(field, halos, out, faces, ts, also=None):
         for t in ts:
             slab, summed = sum0(field, halos, t)
-            fresh = KEEP * slab + g0[t] * (s_ref[t] + summed)
+            fresh = KEEP * slab + g0[PAD0 + t, inner_z] * (s_ref[t] + summed)
             put(out, faces, t, fresh)
             if also is not None:
                 also[t] = fresh
@@ -271,9 +319,12 @@
     sweep0(v0a, y0.at[0], v0b, ys0.at[1], inside)
     finish(over_t)
     sweep0(v0a, y0.at[0], v0b, ys0.at[1], ends)
-    sides, over_t = exchange(1, v0b, ys0.at[1], y0.at[1])
+    for t in range(size_t):
+        ys2[0, t] = v0b[PAD0 + t, inner_z, pl.ds(1, 1)]
+        ys2[1, t] = v0b[PAD0 + t, inner_z, pl.ds(rows - 2, 1)]
+    sides, over_t = exchange(1, v0b)
     finish(mass_copies)
-    for a, b, count in near1(2):
+    for a, b, count in area1(1, 1, 1):
         write1(g1, a, b, DAMPING / (4.0 + read1(m1, a, b, count)))
 
     def to_level2(slabs):
@@ -300,6 +351,7 @@
     finish(over_t)
     remainder0((0, size_t1 - 1))
     source_copies = spread1(1, s1)
+    behind_copies = behind()
     def take(field, places, cells):
         return jnp.stack([field[places[cell]] for cell in cells])
 
@@ -313,12 +365,13 @@
         put3(m3, cells, DAMPING / (1.0 + coarsened3(take(m2, slots, cells))))
     finish(source_copies)
 
-    for a, b, count in near1(2):
+    for a, b, count in area1(1, 1, 0):
         write1(v1a, a, b, read1(g1, a, b, count) * read1(s1, a, b, count))
-    sweep1(v1a, v1b, 1)
+    sweep1(v1a, v1b, (1, 0), (1, 1, 0))
     remainder = []
-    for a, b, count in near1(0):
-        slab, summed = sum1(v1b, a, b, count, held1[1])
+    held = {t: (z, count) for t, z, count in area1(1, 0)}
+    for a, b, count in area1(0):
+        slab, summed = sum1(v1b, a, b, count, held)
         write1(v1h, a, b, slab)
         remainder.append(
             read1(s1, a, b, count) + 0.5 * summed - (4.0 + read1(m1, a, b, count)) * slab
@@ -391,13 +444,13 @@
 
     for t in range(-2, part_t + 2):
         for z in range(-2, part_z + 2):
-            if max(-t, t - part_t + 1, 0) + max(-z, z - part_z + 1, 0) <= 2:
+            if max(-t, t - part_t + 1, 0) + max(-z, z - part_z + 1, 0) <= 3:
                 correct1(t, z)
     finish(wide_copies)
-    for t, z, count in near1(3):
+    for t, z, count in area1(2, 2, 1, 1):
         write1(v1w, t, z, read1(v1h, t, z, count) + e2[t // 2 + 2, pl.ds(z + 2, count)])
-    sweep1(v1w, v1x, 2)
-    sweep1(v1x, e1, 1)
+    sweep1(v1w, v1x, (1, 1, 1), (2, 2, 1, 1))
+    sweep1(v1x, e1, (1, 1), (1, 1, 1))
 
     under = lax.rem(gy + ngy - 1, ngy)
     over = lax.rem(gy + 1, ngy)
@@ -407,33 +460,46 @@
         odd = jnp.where(odd_lane(slab), slab, rolled(slab, -1, 2))
         return jnp.stack([even, odd], axis=1).reshape(2 * slab.shape[0], *slab.shape[1:])
 
-    def corrected0(layers):
-        for t in layers:
-            own = [p for p in (2 * t + 1, 2 * t + 2) if 1 <= p <= size_t]
-            if not own:
-                p = 0 if t < 0 else size_t + 1
-                fine = refined_z(doubled(split1(e1[PAD_T + t, pl.ds(PAD_Z, pairs1), gy]), 0))
-                v0w[p, inner_z] = v0b[p, inner_z] + fine
+    def corrected0(level):
+        fine = split1(e1[PAD_T + level, pl.ds(PAD_Z - 1, pairs1 + 2), gy])[1:-1]
+        fine = refined_z(doubled(fine, level % 4))
+        beyond = [
+            refined_z(split1(e1[PAD_T + level, pl.ds(PAD_Z - 1, pairs1 + 2), side, pl.ds(row, 1)])[1:-1])
+            for side, row in ((under, rows1 - 1), (over, 0))
+        ]
+        for t in (2 * level, 2 * level + 1):
+            reach = 2 - max(-t, t - size_t + 1, 0)
+            out = pl.ds(PAD0 - reach, size_z + 2 * reach)
+            v0w[PAD0 + t, out] = v0b[PAD0 + t, out] + fine[2 - reach:size_z + 2 + reach]
+            reach -= 1
+            if reach < 0:
                 continue
-            fine = split1(e1[PAD_T + t, pl.ds(PAD_Z - 1, pairs1 + 2), gy])
-            fine = refined_z(doubled(fine[1:-1], t % 4))
-            fine = fine[1:1 + size_z + 2]
-            low = refined_z(split1(e1[PAD_T + t, pl.ds(PAD_Z, pairs1), under, pl.ds(rows1 - 1, 1)]))
-            high = refined_z(split1(e1[PAD_T + t, pl.ds(PAD_Z, pairs1), over, pl.ds(0, 1)]))
-            for p in own:
-                v0w[p] = v0b[p] + fine
-                y0[2, 0, p - 1] = y0[1, 0, p - 1] + low
-                y0[2, 1, p - 1] = y0[1, 1, p - 1] + high
-
-    corrected0(range(-1, size_t1 + 1))
-    sweep0(v0w, y0.at[2], v0x, ys0.at[2], range(size_t))
-    sides, over_t = exchange(2, v0x, ys0.at[2], y0.at[3])
-    finish(sides)
-    sweep0(v0x, y0.at[3], v0s, ys0.at[3], inside, sol_ref)
-    finish(over_t)
-    sweep0(v0x, y0.at[3], v0s, ys0.at[3], ends, sol_ref)
+            out = pl.ds(1 - reach, size_z + 2 * reach)
+            for side in range(2):
+                shifted = beyond[side][2 - reach:size_z + 2 + reach]
+                y0[2, side, 1 + t, out] = y0[1, side, 1 + t, out] + shifted
+                if reach == 1:
+                    y2[1, side, t] = y2[0, side, t] + beyond[side][2:size_z + 2]
+
+    finish(behind_copies)
+    for level in range(-1, size_t1 + 1):
+        corrected0(level)
+    for t in range(-1, size_t + 1):
+        reach = 1 if 0 <= t < size_t else 0
+        out = pl.ds(PAD0 - reach, size_z + 2 * reach)
+        slab, summed = sum0(v0w, y0.at[2], t, reach)
+        v0x[PAD0 + t, out] = KEEP * slab + v0a[PAD0 + t, out] + g0[PAD0 + t, out] * summed
+    for t in range(size_t):
+        for side, row in ((0, 0), (1, rows - 1)):
+            at = lambda dt, dz: y0[2, side, 1 + t + dt, pl.ds(1 + dz, size_z)]
+            slab = at(0, 0)
+            summed = at(-1, 0) + at(1, 0) + at(0, -1) + at(0, 1)
+            summed = summed + y2[1, side, t] + v0w[PAD0 + t, inner_z, pl.ds(row, 1)]
+            summed = summed + rolled(slab, 1, 2) + rolled(slab, -1, 2)
+            y0[3, side, 1 + t, own_z] = KEEP * slab + y0[0, side, 1 + t, own_z] + yg[side, t] * summed
+    sweep0(v0x, y0.at[3], v0s, ys0.at[2], range(size_t), sol_ref)
     earlier = len(sent)
-    sides, over_t = exchange(3, v0s, ys0.at[3], y0.at[4])
+    sides, over_t = exchange(2, v0s)
     finish_sends(sent[:earlier])
 
     def residual(ts):
@@ -492,7 +558,8 @@
     sites = lambda cells, steps: grown(cells, steps, 2 * nta, 2 * ngz)
     blocks = lambda cells: {(t // 2, z // 2) for t, z in cells}
     inner = lambda cells: {(2 * t + a, 2 * z + b) for t, z in cells for a in (0, 1) for b in (0, 1)}
-    last = sites(inner({(0, 0)}), 2)
+    box = {(t % (2 * nta), z % (2 * ngz)) for t in range(-2, 4) for z in range(-2, 4)}
+    last = sites(inner({(0, 0)}), 3) & box
     first, base = sites(last, 1), sites(last, 2)
     coarse = [grown(blocks(base), steps, nta, ngz) for steps in range(4)]
     swept = sites(inner(coarse[3]), 1) | base
@@ -511,19 +578,21 @@
     part_t, part_z, rows2 = size_t // 4, size_z // 4, rows // 4
     vmem = lambda *shape: pltpu.VMEM(shape, jnp.float32)
     dma = lambda *shape: pltpu.SemaphoreType.DMA(shape)
-    padded0 = vmem(size_t + 2, size_z + 2, rows, lanes)
+    padded0 = vmem(size_t + 2 * PAD0, size_z + 2 * PAD0, rows, lanes)
+    faces = vmem(2, size_t, size_z, 1, lanes)
     padded1 = vmem(size_t1 + 2 * PAD_T, pairs1 + 2 * PAD_Z, ngy, rows1, lanes)
     window = len(plan(nta, ngz)["source"])
     packs = vmem(window, rows2 * ngy, lanes)
     packs3 = vmem(len(plan(nta, ngz)["coarse"][3]), rows2 * ngy, lanes)
     spreads = 8 * ngy + ngy - 1
     scratch = [
-        vmem(size_t, size_z, rows, lanes), padded0, padded0, padded0, padded0, padded0,
-        vmem(5, 2, size_t, size_z, 1, lanes), vmem(4, 2, size_t, size_z, 1, lanes),
+        *[padded0] * 6,
+        vmem(5, 2, size_t + 2, size_z + 2, 1, lanes), vmem(3, 2, size_t, size_z, 1, lanes),
+        vmem(2, 2, size_t, size_z, 1, lanes), faces, faces, faces,
         vmem(max(size_t1, part_t + 2), size_z, max(rows, ngy * rows1), lanes),
         *[padded1] * 9, vmem(part_t + 4, part_z + 4, ngy * rows1, lanes),
         *[packs] * 5, *[packs3] * 4,
-        dma(4, 6), dma(4, 6), dma(2, spreads), dma(2, spreads), dma(8), dma(8),
+        dma(3, 6), dma(3, 6), dma(24), dma(24), dma(2, spreads), dma(2, spreads), dma(12), dma(12),
         dma(2, window), dma(2, window),
         vmem(size_t, size_z, rows, lanes), vmem(size_t, size_z, rows, lanes), dma(2, size_t),
     ]

time: 53.6 us -> 53.4 us (level)
  no operation moved by 1% of the time
where the time goes in v5:
time: 53.4 us; the launch traced here: 53.2 us
  Pallas kernels  51 us (96%)
  local copies, waits for them, and re-layouts  1.59 us (3%)
  between operations  0.64 us (1%)
    pallas_call x1, Pallas kernels, per_device(): pl.pallas_call(functools.partial(kernel, sizes), out_shape=(block, block)...  51 us
    unnamed x2, local copies, waits for them, and re-layouts  1.59 us

profile of v5, /device:TPU:1, one launch (start us, length us, event | category | flops | bytes accessed | tf_op | source)
XLA Modules:
  0.0 53.2 jit_solution(3038360085268522834)
XLA Ops:
  0.6 51.0 %shard_map.41 = (f32[8,8,16,128]{3,2,1,0:T(8,128)S(1)}, f32[8,8,16,128]{3,2,1,0:T(8,128)S(1)}) custom-call(f32[8,8,16,128]{3,2,1,0:T(8,128)} %s_hbm.1, f32[8,8,16,128]{3,2,1,0:T(8,128)} %m_hbm.1), custom_call_target="tpu_custom_call" | custom-call | tf_op jit(solution)/shard_map/pallas_call | solution.py:600
  51.6 0.8 %copy.6 = f32[8,8,16,128]{3,2,1,0:T(8,128)} copy(f32[8,8,16,128]{3,2,1,0:T(8,128)S(1)} %get-tuple-element.4) | data formatting | bytes 1048576
  52.4 0.8 %copy.7 = f32[8,8,16,128]{3,2,1,0:T(8,128)} copy(f32[8,8,16,128]{3,2,1,0:T(8,128)S(1)} %get-tuple-element.5) | data formatting | bytes 1048576

commit v6 on v5

--- a/solution.py
+++ b/solution.py
@@ -41,7 +41,7 @@
     (g0, v0a, v0b, v0w, v0x, v0s, y0, ys0, y2, ys2, yg, ysg, fold,
      s1, m1, g1, v1a, v1b, v1h, v1w, v1x, e1, e2,
      m2, s2, g2, u2, w2, m3, s3, u3, w3,
-     f0s, f0r, fhs, fhr, f1s, f1r, fxs, fxr, gsend, grecv, s_ref, m_ref, loaded) = scratch
+     s_ref, m_ref, tally, departed, arrived, loaded) = scratch
     size_t, size_z, rows, lanes = s_ref.shape
     size_t1, pairs1, rows1 = size_t // 2, size_z // 4, rows // 2
     part_t, part_z, rows2 = size_t // 4, size_z // 4, rows // 4
@@ -69,42 +69,45 @@
         (cell for cell in slots if cell != (0, 0)),
         key=lambda c: -(abs(centred(c[0], nta)) + 2 * abs(centred(c[1], ngz))),
     )
-    loads = []
-    for t in range(size_t):
-        loads.append((
-            pltpu.make_async_copy(m_hbm.at[pl.ds(t, 1)], m_ref.at[pl.ds(t, 1)], loaded.at[0, t]),
-            pltpu.make_async_copy(s_hbm.at[pl.ds(t, 1)], s_ref.at[pl.ds(t, 1)], loaded.at[1, t]),
-        ))
+    half = size_t // 2
+    loads = [
+        [
+            pltpu.make_async_copy(source.at[pl.ds(part * half, half)], target.at[pl.ds(part * half, half)], loaded.at[part, place])
+            for place, (source, target) in enumerate(((m_hbm, m_ref), (s_hbm, s_ref)))
+        ]
+        for part in range(2)
+    ]
     met = sorted({(dt % nta, dz % ngz, dy % ngy) for dt, dz, dy in near + [(-t, -z, 0) for t, z in across]} - {(0, 0, 0)})
-    for t in [0, size_t - 1] + list(range(1, size_t - 1)):
-        for load in loads[t]:
-            load.start()
+    for load in loads[0] + loads[1]:
+        load.start()
     barrier = pltpu.get_barrier_semaphore()
     for offset in met:
         pl.semaphore_signal(barrier, inc=1, device_id=device(*offset), device_id_type=MESH)
 
-    def send(moves, sends, receives):
-        copies = [
+    rows_of, all_rows = {}, []
+
+    def send(group, moves):
+        for source, target, offset in moves:
             pltpu.make_async_remote_copy(
-                src_ref=source, dst_ref=target, send_sem=sends(place), recv_sem=receives(place),
+                src_ref=source, dst_ref=target, send_sem=departed, recv_sem=arrived.at[group],
                 device_id=device(*offset), device_id_type=MESH,
-            )
-            for place, source, target, offset in moves
-        ]
-        for copy in copies:
-            copy.start()
-        sent.extend(copies)
-        return copies
-
-    def finish(copies):
-        for copy in copies:
-            copy.wait_recv()
-
-    sent = []
-
-    def finish_sends(copies):
-        for copy in copies:
-            copy.wait_send()
+            ).start()
+            count = 1
+            for extent in source.shape[:-1]:
+                count *= extent
+            rows_of[group] = rows_of.get(group, 0) + count
+            all_rows.append(count)
+        return group
+
+    def whole(group, count):
+        view = tally.at[pl.ds(0, count)]
+        return pltpu.make_async_remote_copy(
+            src_ref=view, dst_ref=view, send_sem=departed, recv_sem=arrived.at[group],
+            device_id=device(1, 0, 0), device_id_type=MESH,
+        )
+
+    def finish(group):
+        whole(group, rows_of[group]).wait_recv()
 
     inner_t, inner_z = pl.ds(PAD0, size_t), pl.ds(PAD0, size_z)
 
@@ -124,18 +127,15 @@
         moves = [
             (faces.at[1], halos.at[0, own_t, own_z], (0, 0, 1)), (faces.at[0], halos.at[1, own_t, own_z], (0, 0, -1)),
         ] + faces0(field, 1)
-        copies = send(
-            [(place, *move) for place, move in enumerate(moves)],
-            lambda place: f0s.at[number, place], lambda place: f0r.at[number, place],
-        )
-        return copies[:4], copies[4:]
-
-    def behind():
+        return send(2 * number, moves[:4]), send(2 * number + 1, moves[4:])
+
+    def weights_behind():
+        moves = [(ysg.at[1], yg.at[0], (0, 0, 1)), (ysg.at[0], yg.at[1], (0, 0, -1))]
+        return send(6, moves + faces0(g0, 1))
+
+    def second_behind():
         one = lambda at: pl.ds(at, 1)
-        moves = [
-            (ys2.at[1], y2.at[0, 0], (0, 0, 1)), (ys2.at[0], y2.at[0, 1], (0, 0, -1)),
-            (ysg.at[1], yg.at[0], (0, 0, 1)), (ysg.at[0], yg.at[1], (0, 0, -1)),
-        ]
+        moves = [(ys2.at[1], y2.at[0, 0], (0, 0, 1)), (ys2.at[0], y2.at[0, 1], (0, 0, -1))]
         for up_t in (1, 0):
             for up_z in (1, 0):
                 moves.append((
@@ -154,11 +154,7 @@
                     faces.at[:, one((size_z - 1) * up)], halos.at[own_t, one((size_z + 1) * (1 - up))],
                     (0, 2 * up - 1, 2 * up_y - 1),
                 ))
-        moves += faces0(v0b, 2) + faces0(g0, 1)
-        return send(
-            [(place, *move) for place, move in enumerate(moves)],
-            lambda place: fhs.at[place], lambda place: fhr.at[place],
-        )
+        return send(7, moves + faces0(v0b, 2))
 
     def layers1(deep_t, deep_z, corner_t):
         own_t, own_z = pl.ds(PAD_T, size_t1), pl.ds(PAD_Z, pairs1)
@@ -182,36 +178,32 @@
     def spread1(number, field):
         part = pl.ds(gy, 1)
         own = field.at[pl.ds(PAD_T, size_t1), pl.ds(PAD_Z, pairs1), part]
-        moves = [(8 * ngy + dy - 1, own, own, (0, 0, dy)) for dy in range(1, ngy)]
+        moves = [(own, own, (0, 0, dy)) for dy in range(1, ngy)]
         for dy in reversed(range(ngy)):
-            for place, (here_t, here_z, there_t, there_z, dt, dz) in enumerate(layers1(2, 1, 2)):
-                moves.append((
-                    8 * dy + place, field.at[here_t, here_z, part], field.at[there_t, there_z, part], (dt, dz, dy),
-                ))
-        return send(moves, lambda place: f1s.at[number, place], lambda place: f1r.at[number, place])
+            for here_t, here_z, there_t, there_z, dt, dz in layers1(2, 1, 2):
+                moves.append((field.at[here_t, here_z, part], field.at[there_t, there_z, part], (dt, dz, dy)))
+        return send(8 + number, moves)
 
     def widen1(field):
         moves = [
-            (place, field.at[here_t, here_z], field.at[there_t, there_z], (dt, dz, 0))
-            for place, (here_t, here_z, there_t, there_z, dt, dz) in enumerate(layers1(3, 2, 3))
+            (field.at[here_t, here_z], field.at[there_t, there_z], (dt, dz, 0))
+            for here_t, here_z, there_t, there_z, dt, dz in layers1(3, 2, 3)
         ]
         one = lambda at: pl.ds(at, 1)
         for up in (1, 0):
             for up_z in (1, 0):
                 moves.append((
-                    len(moves),
                     field.at[one(PAD_T + (size_t1 - 1) * up), one(PAD_Z + 1 + (pairs1 - 3) * up_z)],
                     field.at[one(PAD_T - 1 + (size_t1 + 1) * (1 - up)), one(PAD_Z - 2 + (pairs1 + 3) * (1 - up_z))],
                     (2 * up - 1, 2 * up_z - 1, 0),
                 ))
-        return send(moves, lambda place: fxs.at[place], lambda place: fxr.at[place])
+        return send(10, moves)
 
     def gather(number, field):
         own = field.at[slots[0, 0]]
-        return send(
-            [(slots[cell], own, field.at[slots[cell]], (-cell[0], -cell[1], 0)) for cell in across],
-            lambda place: gsend.at[number, place], lambda place: grecv.at[number, place],
-        )
+        return send(11 + number, [
+            (own, field.at[slots[cell]], (-cell[0], -cell[1], 0)) for cell in across
+        ])
 
     def put(field, faces, t, slab):
         field[PAD0 + t, inner_z] = slab
@@ -292,20 +284,20 @@
     inside = list(range(1, size_t - 1))
     ends = [0, size_t - 1]
 
-    def first0(ts):
-        for t in ts:
-            for load in loads[t]:
-                load.wait()
+    for part in range(2):
+        for load in loads[part]:
+            load.wait()
+        for t in range(part * half, (part + 1) * half):
             weight = DAMPING / (8.0 + m_ref[t])
             put(g0, ysg, t, weight)
             put(v0a, ys0.at[0], t, weight * s_ref[t])
 
-    first0(ends + inside)
     pl.semaphore_wait(barrier, len(met))
     sides, over_t = exchange(0, v0a)
     for t in range(size_t1):
         m1[PAD_T + t, pl.ds(PAD_Z, pairs1), gy] = to_level1(m_ref[2 * t] + m_ref[2 * t + 1], t)
     mass_copies = spread1(0, m1)
+    weight_copies = weights_behind()
 
     def sweep0(field, halos, out, faces, ts, also=None):
         for t in ts:
@@ -351,18 +343,12 @@
     finish(over_t)
     remainder0((0, size_t1 - 1))
     source_copies = spread1(1, s1)
-    behind_copies = behind()
     def take(field, places, cells):
         return jnp.stack([field[places[cell]] for cell in cells])
 
     def put3(field, cells, values):
         field[pl.ds(slots3[cells[0]], len(cells))] = values
 
-    finish(mass_copies)
-    for cell in stages["source"]:
-        g2[slots[cell]] = DAMPING / (2.0 + m2[slots[cell]])
-    for cells in batches(stages["coarse"][3], 24):
-        put3(m3, cells, DAMPING / (1.0 + coarsened3(take(m2, slots, cells))))
     finish(source_copies)
 
     for a, b, count in area1(1, 1, 0):
@@ -379,6 +365,12 @@
     packed(s2, to_level2(remainder))
     source_copies = gather(1, s2)
     wide_copies = widen1(v1h)
+    behind_copies = second_behind()
+    finish(mass_copies)
+    for cell in stages["source"]:
+        g2[slots[cell]] = DAMPING / (2.0 + m2[slots[cell]])
+    for cells in batches(stages["coarse"][3], 24):
+        put3(m3, cells, DAMPING / (1.0 + coarsened3(take(m2, slots, cells))))
     finish(source_copies)
 
     def around2(cell):
@@ -481,6 +473,7 @@
                 if reach == 1:
                     y2[1, side, t] = y2[0, side, t] + beyond[side][2:size_z + 2]
 
+    finish(weight_copies)
     finish(behind_copies)
     for level in range(-1, size_t1 + 1):
         corrected0(level)
@@ -498,9 +491,7 @@
             summed = summed + rolled(slab, 1, 2) + rolled(slab, -1, 2)
             y0[3, side, 1 + t, own_z] = KEEP * slab + y0[0, side, 1 + t, own_z] + yg[side, t] * summed
     sweep0(v0x, y0.at[3], v0s, ys0.at[2], range(size_t), sol_ref)
-    earlier = len(sent)
     sides, over_t = exchange(2, v0s)
-    finish_sends(sent[:earlier])
 
     def residual(ts):
         for t in ts:
@@ -511,7 +502,7 @@
     residual(inside)
     finish(over_t)
     residual(ends)
-    finish_sends(sent[earlier:])
+    whole(0, sum(all_rows)).wait_send()
 
 
 def place_in(values, axis):
@@ -584,7 +575,6 @@
     window = len(plan(nta, ngz)["source"])
     packs = vmem(window, rows2 * ngy, lanes)
     packs3 = vmem(len(plan(nta, ngz)["coarse"][3]), rows2 * ngy, lanes)
-    spreads = 8 * ngy + ngy - 1
     scratch = [
         *[padded0] * 6,
         vmem(5, 2, size_t + 2, size_z + 2, 1, lanes), vmem(3, 2, size_t, size_z, 1, lanes),
@@ -592,9 +582,8 @@
         vmem(max(size_t1, part_t + 2), size_z, max(rows, ngy * rows1), lanes),
         *[padded1] * 9, vmem(part_t + 4, part_z + 4, ngy * rows1, lanes),
         *[packs] * 5, *[packs3] * 4,
-        dma(3, 6), dma(3, 6), dma(24), dma(24), dma(2, spreads), dma(2, spreads), dma(12), dma(12),
-        dma(2, window), dma(2, window),
-        vmem(size_t, size_z, rows, lanes), vmem(size_t, size_z, rows, lanes), dma(2, size_t),
+        vmem(size_t, size_z, rows, lanes), vmem(size_t, size_z, rows, lanes),
+        vmem(8192, 1, lanes), pltpu.SemaphoreType.DMA, dma(13), dma(2, 2),
     ]
     block = jax.ShapeDtypeStruct(right_side.shape, jnp.float32)
     return pl.pallas_call(

time: 53.4 us -> 50.3 us (0.942)
  Pallas kernels: 51 us -> 48 us
    pallas_call x1, Pallas kernels: 51 us -> 48 us  [per_device(): pl.pallas_call(functools.partial(kernel, sizes), out_shape=(block, block)...]
where the time goes in v6:
time: 50.3 us; the launch traced here: 50.2 us
  Pallas kernels  48 us (95%)
  local copies, waits for them, and re-layouts  1.59 us (3%)
  between operations  0.64 us (1%)
    pallas_call x1, Pallas kernels, per_device(): pl.pallas_call(functools.partial(kernel, sizes), out_shape=(block, block)...  48 us
    unnamed x2, local copies, waits for them, and re-layouts  1.59 us

profile of v6, /device:TPU:1, one launch (start us, length us, event | category | flops | bytes accessed | tf_op | source)
XLA Modules:
  0.0 50.2 jit_solution(17756414524357445617)
XLA Ops:
  0.6 48.0 %shard_map.41 = (f32[8,8,16,128]{3,2,1,0:T(8,128)S(1)}, f32[8,8,16,128]{3,2,1,0:T(8,128)S(1)}) custom-call(f32[8,8,16,128]{3,2,1,0:T(8,128)} %s_hbm.1, f32[8,8,16,128]{3,2,1,0:T(8,128)} %m_hbm.1), custom_call_target="tpu_custom_call" | custom-call | tf_op jit(solution)/shard_map/pallas_call | solution.py:589
  48.6 0.8 %copy.6 = f32[8,8,16,128]{3,2,1,0:T(8,128)} copy(f32[8,8,16,128]{3,2,1,0:T(8,128)S(1)} %get-tuple-element.4) | data formatting | bytes 1048576
  49.4 0.8 %copy.7 = f32[8,8,16,128]{3,2,1,0:T(8,128)} copy(f32[8,8,16,128]{3,2,1,0:T(8,128)S(1)} %get-tuple-element.5) | data formatting | bytes 1048576

commit v7 on v6

--- a/solution.py
+++ b/solution.py
@@ -77,12 +77,13 @@
         ]
         for part in range(2)
     ]
-    met = sorted({(dt % nta, dz % ngz, dy % ngy) for dt, dz, dy in near + [(-t, -z, 0) for t, z in across]} - {(0, 0, 0)})
-    for load in loads[0] + loads[1]:
-        load.start()
+    met = {(dt % nta, dz % ngz, dy % ngy) for dt, dz, dy in near + [(-t, -z, 0) for t, z in across]} - {(0, 0, 0)}
+    met = sorted(met, key=lambda d: (-abs(centred(d[0], nta)) - 2 * abs(centred(d[1], ngz)) - 2 * d[2], d))
     barrier = pltpu.get_barrier_semaphore()
     for offset in met:
         pl.semaphore_signal(barrier, inc=1, device_id=device(*offset), device_id_type=MESH)
+    for load in loads[0] + loads[1]:
+        load.start()
 
     rows_of, all_rows = {}, []
 
@@ -297,7 +298,6 @@
     for t in range(size_t1):
         m1[PAD_T + t, pl.ds(PAD_Z, pairs1), gy] = to_level1(m_ref[2 * t] + m_ref[2 * t + 1], t)
     mass_copies = spread1(0, m1)
-    weight_copies = weights_behind()
 
     def sweep0(field, halos, out, faces, ts, also=None):
         for t in ts:
@@ -327,8 +327,7 @@
             out.append((summed + pair_swap(summed, 2, 2)) * 0.0625)
         return out
 
-    packed(m2, to_level2([read1(m1, t, 0, pairs1) for t in range(size_t1)]))
-    mass_copies = gather(0, m2)
+    weight_copies = weights_behind()
 
     def remainder0(ts):
         for t in ts:
@@ -343,6 +342,8 @@
     finish(over_t)
     remainder0((0, size_t1 - 1))
     source_copies = spread1(1, s1)
+    packed(m2, to_level2([read1(m1, t, 0, pairs1) for t in range(size_t1)]))
+    mass_copies = gather(0, m2)
     def take(field, places, cells):
         return jnp.stack([field[places[cell]] for cell in cells])
 

time: 50.3 us -> 49.2 us (0.978)
  Pallas kernels: 48 us -> 46.9 us
    pallas_call x1, Pallas kernels: 48 us -> 46.9 us  [per_device(): pl.pallas_call(functools.partial(kernel, sizes), out_shape=(block, block)...]
where the time goes in v7:
time: 49.2 us; the launch traced here: 49.1 us
  Pallas kernels  46.9 us (95%)
  local copies, waits for them, and re-layouts  1.59 us (3%)
  between operations  0.64 us (1%)
    pallas_call x1, Pallas kernels, per_device(): pl.pallas_call(functools.partial(kernel, sizes), out_shape=(block, block)...  46.9 us
    unnamed x2, local copies, waits for them, and re-layouts  1.59 us

profile of v7, /device:TPU:1, one launch (start us, length us, event | category | flops | bytes accessed | tf_op | source)
XLA Modules:
  0.0 49.1 jit_solution(15535043050998900437)
XLA Ops:
  0.6 46.9 %shard_map.41 = (f32[8,8,16,128]{3,2,1,0:T(8,128)S(1)}, f32[8,8,16,128]{3,2,1,0:T(8,128)S(1)}) custom-call(f32[8,8,16,128]{3,2,1,0:T(8,128)} %s_hbm.1, f32[8,8,16,128]{3,2,1,0:T(8,128)} %m_hbm.1), custom_call_target="tpu_custom_call" | custom-call | tf_op jit(solution)/shard_map/pallas_call | solution.py:590
  47.5 0.8 %copy.6 = f32[8,8,16,128]{3,2,1,0:T(8,128)} copy(f32[8,8,16,128]{3,2,1,0:T(8,128)S(1)} %get-tuple-element.4) | data formatting | bytes 1048576
  48.3 0.8 %copy.7 = f32[8,8,16,128]{3,2,1,0:T(8,128)} copy(f32[8,8,16,128]{3,2,1,0:T(8,128)S(1)} %get-tuple-element.5) | data formatting | bytes 1048576

commit v8 on v7

--- a/solution.py
+++ b/solution.py
@@ -36,9 +36,35 @@
     return jnp.repeat(slab, 2, axis=0)
 
 
-def kernel(sizes, s_hbm, m_hbm, sol_ref, res_ref, *scratch):
+def neighbours0(field, low, high, t, start=0, count=None):
+    count = count or field.shape[1] - 2 * PAD0
+    at = lambda dt, dz: field[PAD0 + t + dt, pl.ds(PAD0 + start + dz, count)]
+    slab = at(0, 0)
+    row = lax.broadcasted_iota(jnp.int32, slab.shape, 1)
+    summed = at(-1, 0) + at(1, 0) + at(0, -1) + at(0, 1)
+    summed = summed + jnp.where(row == 0, low, rolled(slab, 1, 1))
+    summed = summed + jnp.where(row == slab.shape[1] - 1, high, rolled(slab, -1, 1))
+    return slab, summed + rolled(slab, 1, 2) + rolled(slab, -1, 2)
+
+
+def last_kernel(v0s, yl, base, sol_hbm, res_hbm, res, written):
+    size_t, size_z = base.shape[:2]
+    copies = [pltpu.make_async_copy(v0s.at[pl.ds(PAD0, size_t), pl.ds(PAD0, size_z)], sol_hbm, written.at[0])]
+    copies[0].start()
+    for part in range(2):
+        own = pl.ds(part * (size_t // 2), size_t // 2)
+        for t in range(part * (size_t // 2), (part + 1) * (size_t // 2)):
+            _, summed = neighbours0(v0s, yl[0, t], yl[1, t], t)
+            res[t] = base[t] + summed
+        copies.append(pltpu.make_async_copy(res.at[own], res_hbm.at[own], written.at[1 + part]))
+        copies[-1].start()
+    for copy in copies:
+        copy.wait()
+
+
+def kernel(sizes, s_hbm, m_hbm, v0s, yl, base, *scratch):
     nta, ngz, ngy = sizes
-    (g0, v0a, v0b, v0w, v0x, v0s, y0, ys0, y2, ys2, yg, ysg, fold,
+    (g0, v0a, v0b, v0w, v0x, y0, ys0, y2, ys2, yg, ysg, fold,
      s1, m1, g1, v1a, v1b, v1h, v1w, v1x, e1, e2,
      m2, s2, g2, u2, w2, m3, s3, u3, w3,
      s_ref, m_ref, tally, departed, arrived, loaded) = scratch
@@ -124,10 +150,9 @@
     own_t, own_z = pl.ds(1, size_t), pl.ds(1, size_z)
 
     def exchange(number, field):
-        faces, halos = ys0.at[number], y0.at[(0, 1, 4)[number]]
-        moves = [
-            (faces.at[1], halos.at[0, own_t, own_z], (0, 0, 1)), (faces.at[0], halos.at[1, own_t, own_z], (0, 0, -1)),
-        ] + faces0(field, 1)
+        faces = ys0.at[number]
+        low, high = [y0.at[number, side, own_t, own_z] if number < 2 else yl.at[side] for side in range(2)]
+        moves = [(faces.at[1], low, (0, 0, 1)), (faces.at[0], high, (0, 0, -1))] + faces0(field, 1)
         return send(2 * number, moves[:4]), send(2 * number + 1, moves[4:])
 
     def weights_behind():
@@ -213,13 +238,8 @@
 
     def sum0(field, halos, t, reach=0):
         count = size_z + 2 * reach
-        at = lambda dt, dz: field[PAD0 + t + dt, pl.ds(PAD0 - reach + dz, count)]
-        slab, out = at(0, 0), pl.ds(1 - reach, count)
-        row = lax.broadcasted_iota(jnp.int32, slab.shape, 1)
-        summed = at(-1, 0) + at(1, 0) + at(0, -1) + at(0, 1)
-        summed = summed + jnp.where(row == 0, halos[0, 1 + t, out], rolled(slab, 1, 1))
-        summed = summed + jnp.where(row == rows - 1, halos[1, 1 + t, out], rolled(slab, -1, 1))
-        return slab, summed + rolled(slab, 1, 2) + rolled(slab, -1, 2)
+        out = pl.ds(1 - reach, count)
+        return neighbours0(field, halos[0, 1 + t, out], halos[1, 1 + t, out], t, -reach, count)
 
     def folded(summed, place):
         count, high, _ = summed.shape
@@ -299,13 +319,11 @@
         m1[PAD_T + t, pl.ds(PAD_Z, pairs1), gy] = to_level1(m_ref[2 * t] + m_ref[2 * t + 1], t)
     mass_copies = spread1(0, m1)
 
-    def sweep0(field, halos, out, faces, ts, also=None):
+    def sweep0(field, halos, out, faces, ts):
         for t in ts:
             slab, summed = sum0(field, halos, t)
             fresh = KEEP * slab + g0[PAD0 + t, inner_z] * (s_ref[t] + summed)
             put(out, faces, t, fresh)
-            if also is not None:
-                also[t] = fresh
 
     finish(sides)
     sweep0(v0a, y0.at[0], v0b, ys0.at[1], inside)
@@ -491,18 +509,13 @@
             summed = summed + y2[1, side, t] + v0w[PAD0 + t, inner_z, pl.ds(row, 1)]
             summed = summed + rolled(slab, 1, 2) + rolled(slab, -1, 2)
             y0[3, side, 1 + t, own_z] = KEEP * slab + y0[0, side, 1 + t, own_z] + yg[side, t] * summed
-    sweep0(v0x, y0.at[3], v0s, ys0.at[2], range(size_t), sol_ref)
+    sweep0(v0x, y0.at[3], v0s, ys0.at[2], range(size_t))
     sides, over_t = exchange(2, v0s)
 
-    def residual(ts):
-        for t in ts:
-            slab, summed = sum0(v0s, y0.at[4], t)
-            res_ref[t] = s_ref[t] + summed - (8.0 + m_ref[t]) * slab
-
+    for t in range(size_t):
+        base[t] = s_ref[t] - (8.0 + m_ref[t]) * v0s[PAD0 + t, inner_z]
     finish(sides)
-    residual(inside)
     finish(over_t)
-    residual(ends)
     whole(0, sum(all_rows)).wait_send()
 
 
@@ -577,8 +590,8 @@
     packs = vmem(window, rows2 * ngy, lanes)
     packs3 = vmem(len(plan(nta, ngz)["coarse"][3]), rows2 * ngy, lanes)
     scratch = [
-        *[padded0] * 6,
-        vmem(5, 2, size_t + 2, size_z + 2, 1, lanes), vmem(3, 2, size_t, size_z, 1, lanes),
+        *[padded0] * 5,
+        vmem(4, 2, size_t + 2, size_z + 2, 1, lanes), vmem(3, 2, size_t, size_z, 1, lanes),
         vmem(2, 2, size_t, size_z, 1, lanes), faces, faces, faces,
         vmem(max(size_t1, part_t + 2), size_z, max(rows, ngy * rows1), lanes),
         *[padded1] * 9, vmem(part_t + 4, part_z + 4, ngy * rows1, lanes),
@@ -586,17 +599,28 @@
         vmem(size_t, size_z, rows, lanes), vmem(size_t, size_z, rows, lanes),
         vmem(8192, 1, lanes), pltpu.SemaphoreType.DMA, dma(13), dma(2, 2),
     ]
-    block = jax.ShapeDtypeStruct(right_side.shape, jnp.float32)
-    return pl.pallas_call(
+    array = lambda *shape: jax.ShapeDtypeStruct(shape, jnp.float32)
+    block, place = array(*right_side.shape), pl.BlockSpec(memory_space=pltpu.VMEM)
+    kept = pl.pallas_call(
         functools.partial(kernel, sizes),
-        out_shape=(block, block),
+        out_shape=(
+            array(size_t + 2 * PAD0, size_z + 2 * PAD0, rows, lanes), array(2, size_t, size_z, 1, lanes), block,
+        ),
         in_specs=[pl.BlockSpec(memory_space=pltpu.HBM)] * 2,
-        out_specs=(pl.BlockSpec(memory_space=pltpu.VMEM),) * 2,
+        out_specs=(place,) * 3,
         scratch_shapes=scratch,
         compiler_params=pltpu.CompilerParams(
             collective_id=0, has_side_effects=True, vmem_limit_bytes=48 * 1024 * 1024
         ),
     )(*[pltpu.with_memory_space_constraint(values, pltpu.HBM) for values in (right_side, mass_field)])
+    return pl.pallas_call(
+        last_kernel,
+        out_shape=(block, block),
+        in_specs=[place] * 3,
+        out_specs=(pl.BlockSpec(memory_space=pltpu.HBM),) * 2,
+        scratch_shapes=[vmem(size_t, size_z, rows, lanes), dma(3)],
+        compiler_params=pltpu.CompilerParams(vmem_limit_bytes=8 * 1024 * 1024),
+    )(*kept)
 
 
 def solution(mesh):

time: 49.2 us -> 48.4 us (0.984)
  local copies, waits for them, and re-layouts: 1.59 us -> 0 us
  Pallas kernels: 46.9 us -> 47.7 us
    unnamed x2 -> x0, local copies, waits for them, and re-layouts: 1.59 us -> none
    pallas_call x1 -> x2, Pallas kernels: 46.9 us -> 47.7 us  [the longest x1 46.6 us: per_device(): pl.pallas_call(functools.partial(kernel, sizes), out_shape=(array(size_t...]
where the time goes in v8:
time: 48.4 us; the launch traced here: 48.3 us
  Pallas kernels  47.7 us (99%)
  between operations  0.64 us (1%)
    pallas_call x1, Pallas kernels, per_device(): pl.pallas_call(functools.partial(kernel, sizes), out_shape=(array(size_t...  46.6 us
    pallas_call x1, Pallas kernels, per_device(): pl.pallas_call(last_kernel, out_shape=(block, block), in_specs=[place] *...  1.09 us

profile of v8, /device:TPU:1, one launch (start us, length us, event | category | flops | bytes accessed | tf_op | source)
XLA Modules:
  0.0 48.3 jit_solution(13152944296693288853)
XLA Ops:
  0.6 46.6 %shard_map.41 = (f32[12,12,16,128]{3,2,1,0:T(8,128)S(1)}, f32[2,8,8,1,128]{4,3,2,1,0:T(1,128)S(1)}, f32[8,8,16,128]{3,2,1,0:T(8,128)S(1)}) custom-call(f32[8,8,16,128]{3,2,1,0:T(8,128)} %s_hbm.1, f32[8,8,16,128]{3,2,1,0:T(8,128)} %m_hbm.1), custom_call_target="tpu_custom_call" | custom-call | tf_op jit(solution)/shard_map/pallas_call | solution.py:604
  47.3 1.1 %shard_map.42 = (f32[8,8,16,128]{3,2,1,0:T(8,128)}, f32[8,8,16,128]{3,2,1,0:T(8,128)}) custom-call(f32[12,12,16,128]{3,2,1,0:T(8,128)S(1)} %get-tuple-element.5.v0s, f32[2,8,8,1,128]{4,3,2,1,0:T(1,128)S(1)} %get-tuple-element.6.yl, f32[8,8,16,128]{3,2,1,0:T(8,128)S(1)} %get-tuple-element.7.base), custom_call_target="tpu_custom_call" | custom-call | tf_op jit(solution)/shard_map/pallas_call | solution.py:616

commit v9 on v8

--- a/solution.py
+++ b/solution.py
@@ -117,7 +117,7 @@
         for source, target, offset in moves:
             pltpu.make_async_remote_copy(
                 src_ref=source, dst_ref=target, send_sem=departed, recv_sem=arrived.at[group],
-                device_id=device(*offset), device_id_type=MESH,
+                device_id=offset if isinstance(offset, dict) else device(*offset), device_id_type=MESH,
             ).start()
             count = 1
             for extent in source.shape[:-1]:
@@ -225,10 +225,22 @@
                 ))
         return send(10, moves)
 
-    def gather(number, field):
+    def gather(number, field, cells):
         own = field.at[slots[0, 0]]
-        return send(11 + number, [
-            (own, field.at[slots[cell]], (-cell[0], -cell[1], 0)) for cell in across
+        return send(11 + number, [(own, field.at[slots[cell]], (-cell[0], -cell[1], 0)) for cell in cells])
+
+    core = lax.rem(ta, 2)
+    even = [cell for cell in across if cell[0] % 2 == 0]
+
+    def relay(field):
+        sibling = {"ta": ta + 1 - 2 * core, "gz": gz, "gy": gy}
+        count = len(slots) // ngz // 2
+        return send(13, [
+            (
+                field.at[pl.ds((2 * number + 2 - 2 * core) * ngz, ngz)],
+                field.at[pl.ds((2 * number + 1) * ngz, ngz)], sibling,
+            )
+            for number in range(count)
         ])
 
     def put(field, faces, t, slab):
@@ -361,7 +373,7 @@
     remainder0((0, size_t1 - 1))
     source_copies = spread1(1, s1)
     packed(m2, to_level2([read1(m1, t, 0, pairs1) for t in range(size_t1)]))
-    mass_copies = gather(0, m2)
+    mass_copies = gather(0, m2, even)
     def take(field, places, cells):
         return jnp.stack([field[places[cell]] for cell in cells])
 
@@ -382,8 +394,10 @@
             read1(s1, a, b, count) + 0.5 * summed - (4.0 + read1(m1, a, b, count)) * slab
         )
     packed(s2, to_level2(remainder))
-    source_copies = gather(1, s2)
+    source_copies = gather(1, s2, across)
     wide_copies = widen1(v1h)
+    finish(mass_copies)
+    mass_copies = relay(m2)
     behind_copies = second_behind()
     finish(mass_copies)
     for cell in stages["source"]:
@@ -597,7 +611,7 @@
         *[padded1] * 9, vmem(part_t + 4, part_z + 4, ngy * rows1, lanes),
         *[packs] * 5, *[packs3] * 4,
         vmem(size_t, size_z, rows, lanes), vmem(size_t, size_z, rows, lanes),
-        vmem(8192, 1, lanes), pltpu.SemaphoreType.DMA, dma(13), dma(2, 2),
+        vmem(8192, 1, lanes), pltpu.SemaphoreType.DMA, dma(15), dma(2, 2),
     ]
     array = lambda *shape: jax.ShapeDtypeStruct(shape, jnp.float32)
     block, place = array(*right_side.shape), pl.BlockSpec(memory_space=pltpu.VMEM)

time: 48.4 us -> 47.8 us (0.988)
  Pallas kernels: 47.7 us -> 47 us
    pallas_call x1, Pallas kernels: 46.6 us -> 46 us  [per_device(): pl.pallas_call(functools.partial(kernel, sizes), out_shape=(array(size_t...]
where the time goes in v9:
time: 47.8 us; the launch traced here: 47.7 us
  Pallas kernels  47 us (98%)
  between operations  0.64 us (1%)
    pallas_call x1, Pallas kernels, per_device(): pl.pallas_call(functools.partial(kernel, sizes), out_shape=(array(size_t...  46 us
    pallas_call x1, Pallas kernels, per_device(): pl.pallas_call(last_kernel, out_shape=(block, block), in_specs=[place] *...  1.09 us

profile of v9, /device:TPU:1, one launch (start us, length us, event | category | flops | bytes accessed | tf_op | source)
XLA Modules:
  0.0 47.7 jit_solution(9998372096340595269)
XLA Ops:
  0.6 46.0 %shard_map.41 = (f32[12,12,16,128]{3,2,1,0:T(8,128)S(1)}, f32[2,8,8,1,128]{4,3,2,1,0:T(1,128)S(1)}, f32[8,8,16,128]{3,2,1,0:T(8,128)S(1)}) custom-call(f32[8,8,16,128]{3,2,1,0:T(8,128)} %s_hbm.1, f32[8,8,16,128]{3,2,1,0:T(8,128)} %m_hbm.1), custom_call_target="tpu_custom_call" | custom-call | tf_op jit(solution)/shard_map/pallas_call | solution.py:618
  46.6 1.1 %shard_map.42 = (f32[8,8,16,128]{3,2,1,0:T(8,128)}, f32[8,8,16,128]{3,2,1,0:T(8,128)}) custom-call(f32[12,12,16,128]{3,2,1,0:T(8,128)S(1)} %get-tuple-element.5.v0s, f32[2,8,8,1,128]{4,3,2,1,0:T(1,128)S(1)} %get-tuple-element.6.yl, f32[8,8,16,128]{3,2,1,0:T(8,128)S(1)} %get-tuple-element.7.base), custom_call_target="tpu_custom_call" | custom-call | tf_op jit(solution)/shard_map/pallas_call | solution.py:630

commit v10 on v9

--- a/solution.py
+++ b/solution.py
@@ -329,7 +329,6 @@
     sides, over_t = exchange(0, v0a)
     for t in range(size_t1):
         m1[PAD_T + t, pl.ds(PAD_Z, pairs1), gy] = to_level1(m_ref[2 * t] + m_ref[2 * t + 1], t)
-    mass_copies = spread1(0, m1)
 
     def sweep0(field, halos, out, faces, ts):
         for t in ts:
@@ -345,9 +344,7 @@
         ys2[0, t] = v0b[PAD0 + t, inner_z, pl.ds(1, 1)]
         ys2[1, t] = v0b[PAD0 + t, inner_z, pl.ds(rows - 2, 1)]
     sides, over_t = exchange(1, v0b)
-    finish(mass_copies)
-    for a, b, count in area1(1, 1, 1):
-        write1(g1, a, b, DAMPING / (4.0 + read1(m1, a, b, count)))
+    mass_copies = spread1(0, m1)
 
     def to_level2(slabs):
         out = []
@@ -357,7 +354,6 @@
             out.append((summed + pair_swap(summed, 2, 2)) * 0.0625)
         return out
 
-    weight_copies = weights_behind()
 
     def remainder0(ts):
         for t in ts:
@@ -372,8 +368,12 @@
     finish(over_t)
     remainder0((0, size_t1 - 1))
     source_copies = spread1(1, s1)
+    finish(mass_copies)
+    for a, b, count in area1(1, 1, 1):
+        write1(g1, a, b, DAMPING / (4.0 + read1(m1, a, b, count)))
     packed(m2, to_level2([read1(m1, t, 0, pairs1) for t in range(size_t1)]))
     mass_copies = gather(0, m2, even)
+    weight_copies = weights_behind()
     def take(field, places, cells):
         return jnp.stack([field[places[cell]] for cell in cells])
 

time: 47.8 us -> 47.4 us (level)
  no operation moved by 1% of the time
where the time goes in v10:
time: 47.4 us; the launch traced here: 47.3 us
  Pallas kernels  46.7 us (99%)
  between operations  0.64 us (1%)
    pallas_call x1, Pallas kernels, per_device(): pl.pallas_call(functools.partial(kernel, sizes), out_shape=(array(size_t...  45.6 us
    pallas_call x1, Pallas kernels, per_device(): pl.pallas_call(last_kernel, out_shape=(block, block), in_specs=[place] *...  1.09 us

profile of v10, /device:TPU:1, one launch (start us, length us, event | category | flops | bytes accessed | tf_op | source)
XLA Modules:
  0.0 47.3 jit_solution(15954584581754712328)
XLA Ops:
  0.6 45.6 %shard_map.41 = (f32[12,12,16,128]{3,2,1,0:T(8,128)S(1)}, f32[2,8,8,1,128]{4,3,2,1,0:T(1,128)S(1)}, f32[8,8,16,128]{3,2,1,0:T(8,128)S(1)}) custom-call(f32[8,8,16,128]{3,2,1,0:T(8,128)} %s_hbm.1, f32[8,8,16,128]{3,2,1,0:T(8,128)} %m_hbm.1), custom_call_target="tpu_custom_call" | custom-call | tf_op jit(solution)/shard_map/pallas_call | solution.py:618
  46.2 1.1 %shard_map.42 = (f32[8,8,16,128]{3,2,1,0:T(8,128)}, f32[8,8,16,128]{3,2,1,0:T(8,128)}) custom-call(f32[12,12,16,128]{3,2,1,0:T(8,128)S(1)} %get-tuple-element.5.v0s, f32[2,8,8,1,128]{4,3,2,1,0:T(1,128)S(1)} %get-tuple-element.6.yl, f32[8,8,16,128]{3,2,1,0:T(8,128)S(1)} %get-tuple-element.7.base), custom_call_target="tpu_custom_call" | custom-call | tf_op jit(solution)/shard_map/pallas_call | solution.py:630

commit v11 on v10

--- a/solution.py
+++ b/solution.py
@@ -51,9 +51,10 @@
     size_t, size_z = base.shape[:2]
     copies = [pltpu.make_async_copy(v0s.at[pl.ds(PAD0, size_t), pl.ds(PAD0, size_z)], sol_hbm, written.at[0])]
     copies[0].start()
-    for part in range(2):
-        own = pl.ds(part * (size_t // 2), size_t // 2)
-        for t in range(part * (size_t // 2), (part + 1) * (size_t // 2)):
+    quarter = size_t // 4
+    for part in range(4):
+        own = pl.ds(part * quarter, quarter)
+        for t in range(part * quarter, (part + 1) * quarter):
             _, summed = neighbours0(v0s, yl[0, t], yl[1, t], t)
             res[t] = base[t] + summed
         copies.append(pltpu.make_async_copy(res.at[own], res_hbm.at[own], written.at[1 + part]))
@@ -73,7 +74,16 @@
     part_t, part_z, rows2 = size_t // 4, size_z // 4, rows // 4
     stages = plan(nta, ngz)
     slots = {cell: number for number, cell in enumerate(stages["source"])}
-    slots3 = {cell: number for number, cell in enumerate(stages["coarse"][3])}
+    centred = lambda d, n: (d + n // 2) % n - n // 2
+    around2 = lambda cell: [
+        ((cell[0] + dt) % nta, (cell[1] + dz) % ngz) for dt, dz in ((-1, 0), (1, 0), (0, -1), (0, 1))
+    ]
+    close = {cell for cell in slots if abs(centred(cell[0], nta)) <= 4}
+    early2 = [cell for cell in stages["swept"] if {cell, *around2(cell)} & set(slots) <= close]
+    late2 = [cell for cell in stages["swept"] if cell not in early2]
+    early3 = [cell for cell in stages["coarse"][3] if not {cell, *around2(cell)} & set(late2)]
+    late3 = [cell for cell in stages["coarse"][3] if cell not in early3]
+    slots3 = {cell: number for number, cell in enumerate(early3 + late3)}
     ta, gz, gy = lax.axis_index("ta"), lax.axis_index("gz"), lax.axis_index("gy")
 
     places = {}
@@ -90,7 +100,6 @@
         }
 
     near = [(dt, dz, dy) for dt in (-1, 0, 1) for dz in (-1, 0, 1) for dy in range(ngy)]
-    centred = lambda d, n: (d + n // 2) % n - n // 2
     across = sorted(
         (cell for cell in slots if cell != (0, 0)),
         key=lambda c: -(abs(centred(c[0], nta)) + 2 * abs(centred(c[1], ngz))),
@@ -204,10 +213,12 @@
     def spread1(number, field):
         part = pl.ds(gy, 1)
         own = field.at[pl.ds(PAD_T, size_t1), pl.ds(PAD_Z, pairs1), part]
-        moves = [(own, own, (0, 0, dy)) for dy in range(1, ngy)]
-        for dy in reversed(range(ngy)):
-            for here_t, here_z, there_t, there_z, dt, dz in layers1(2, 1, 2):
-                moves.append((field.at[here_t, here_z, part], field.at[there_t, there_z, part], (dt, dz, dy)))
+        spread = [
+            (field.at[here_t, here_z, part], field.at[there_t, there_z, part], (dt, dz, dy))
+            for dy in reversed(range(ngy)) for here_t, here_z, there_t, there_z, dt, dz in layers1(2, 1, 2)
+        ]
+        pair = [(own, own, (0, 0, dy)) for dy in range(1, ngy)]
+        moves = spread[:4] + pair + spread[4:]
         return send(8 + number, moves)
 
     def widen1(field):
@@ -225,9 +236,9 @@
                 ))
         return send(10, moves)
 
-    def gather(number, field, cells):
+    def gather(group, field, cells):
         own = field.at[slots[0, 0]]
-        return send(11 + number, [(own, field.at[slots[cell]], (-cell[0], -cell[1], 0)) for cell in cells])
+        return send(group, [(own, field.at[slots[cell]], (-cell[0], -cell[1], 0)) for cell in cells])
 
     core = lax.rem(ta, 2)
     even = [cell for cell in across if cell[0] % 2 == 0]
@@ -372,7 +383,7 @@
     for a, b, count in area1(1, 1, 1):
         write1(g1, a, b, DAMPING / (4.0 + read1(m1, a, b, count)))
     packed(m2, to_level2([read1(m1, t, 0, pairs1) for t in range(size_t1)]))
-    mass_copies = gather(0, m2, even)
+    mass_copies = gather(11, m2, even)
     weight_copies = weights_behind()
     def take(field, places, cells):
         return jnp.stack([field[places[cell]] for cell in cells])
@@ -394,7 +405,8 @@
             read1(s1, a, b, count) + 0.5 * summed - (4.0 + read1(m1, a, b, count)) * slab
         )
     packed(s2, to_level2(remainder))
-    source_copies = gather(1, s2, across)
+    late_copies = gather(12, s2, [cell for cell in across if cell not in close])
+    source_copies = gather(14, s2, [cell for cell in across if cell in close])
     wide_copies = widen1(v1h)
     finish(mass_copies)
     mass_copies = relay(m2)
@@ -402,13 +414,8 @@
     finish(mass_copies)
     for cell in stages["source"]:
         g2[slots[cell]] = DAMPING / (2.0 + m2[slots[cell]])
-    for cells in batches(stages["coarse"][3], 24):
+    for cells in batches(early3 + late3, 24):
         put3(m3, cells, DAMPING / (1.0 + coarsened3(take(m2, slots, cells))))
-    finish(source_copies)
-
-    def around2(cell):
-        t, z = cell
-        return [((t + dt) % nta, (z + dz) % ngz) for dt, dz in ((-1, 0), (1, 0), (0, -1), (0, 1))]
 
     def sum2(field, cell):
         slab = field[slots[cell]]
@@ -427,19 +434,25 @@
             at = slots[cell]
             out[at] = KEEP * slab + g2[at] * (s2[at] + 0.25 * summed)
 
-    for cell in stages["source"]:
-        at = slots[cell]
-        u2[at] = g2[at] * s2[at]
-        w2[at] = u2[at]
-    sweep2(u2, w2, stages["swept"])
-    for cell in stages["coarse"][3]:
-        slab, summed = sum2(w2, cell)
-        at = slots[cell]
-        s3[slots3[cell]] = s2[at] + 0.25 * summed - (2.0 + m2[at]) * slab
-    for cells in batches(stages["coarse"][3], 24):
-        source = coarsened3(take(s3, slots3, cells))
-        put3(s3, cells, source)
-        put3(u3, cells, take(m3, slots3, cells) * source)
+    def down(cells, swept, coarse):
+        for cell in cells:
+            at = slots[cell]
+            u2[at] = g2[at] * s2[at]
+            w2[at] = u2[at]
+        sweep2(u2, w2, swept)
+        for cell in coarse:
+            slab, summed = sum2(w2, cell)
+            at = slots[cell]
+            s3[slots3[cell]] = s2[at] + 0.25 * summed - (2.0 + m2[at]) * slab
+        for part in batches(coarse, 24):
+            source = coarsened3(take(s3, slots3, part))
+            put3(s3, part, source)
+            put3(u3, part, take(m3, slots3, part) * source)
+
+    finish(source_copies)
+    down([cell for cell in slots if cell in close], early2, early3)
+    finish(late_copies)
+    down([cell for cell in slots if cell not in close], late2, late3)
     old, new = u3, w3
     for steps in (2, 1, 0):
         for cells in batches(stages["coarse"][steps], 13):
@@ -632,7 +645,7 @@
         out_shape=(block, block),
         in_specs=[place] * 3,
         out_specs=(pl.BlockSpec(memory_space=pltpu.HBM),) * 2,
-        scratch_shapes=[vmem(size_t, size_z, rows, lanes), dma(3)],
+        scratch_shapes=[vmem(size_t, size_z, rows, lanes), dma(5)],
         compiler_params=pltpu.CompilerParams(vmem_limit_bytes=8 * 1024 * 1024),
     )(*kept)
 

time: 47.4 us -> 47.5 us (level)
  no operation moved by 1% of the time
where the time goes in v11:
time: 47.5 us; the launch traced here: 47.4 us
  Pallas kernels  46.7 us (98%)
  between operations  0.64 us (1%)
    pallas_call x1, Pallas kernels, per_device(): pl.pallas_call(functools.partial(kernel, sizes), out_shape=(array(size_t...  45.7 us
    pallas_call x1, Pallas kernels, per_device(): pl.pallas_call(last_kernel, out_shape=(block, block), in_specs=[place] *...  1.06 us

profile of v11, /device:TPU:1, one launch (start us, length us, event | category | flops | bytes accessed | tf_op | source)
XLA Modules:
  0.0 47.4 jit_solution(13196686507893685201)
XLA Ops:
  0.6 45.7 %shard_map.41 = (f32[12,12,16,128]{3,2,1,0:T(8,128)S(1)}, f32[2,8,8,1,128]{4,3,2,1,0:T(1,128)S(1)}, f32[8,8,16,128]{3,2,1,0:T(8,128)S(1)}) custom-call(f32[8,8,16,128]{3,2,1,0:T(8,128)} %s_hbm.1, f32[8,8,16,128]{3,2,1,0:T(8,128)} %m_hbm.1), custom_call_target="tpu_custom_call" | custom-call | tf_op jit(solution)/shard_map/pallas_call | solution.py:631
  46.3 1.1 %shard_map.42 = (f32[8,8,16,128]{3,2,1,0:T(8,128)}, f32[8,8,16,128]{3,2,1,0:T(8,128)}) custom-call(f32[12,12,16,128]{3,2,1,0:T(8,128)S(1)} %get-tuple-element.5.v0s, f32[2,8,8,1,128]{4,3,2,1,0:T(1,128)S(1)} %get-tuple-element.6.yl, f32[8,8,16,128]{3,2,1,0:T(8,128)S(1)} %get-tuple-element.7.base), custom_call_target="tpu_custom_call" | custom-call | tf_op jit(solution)/shard_map/pallas_call | solution.py:643
